TPU v7x, 256 devices: a whole 4x4x8 slice. The times are simulated.
256 devices in a mesh: nodes: 128 (over z, x, y), feat: 2 (over core).
Axes of the slice: x: 4, y: 4, z: 8, core: 2. Of those that a mesh axis runs over, the one named last changes fastest.
Arguments:
- grid_latent: bfloat16 [131072, 512], P('nodes', 'feat'), may hold values from -6 to 6
- mesh_latent: bfloat16 [131072, 512], P('nodes', 'feat'), may hold values from -6 to 6
- grid_order: int32 [128, 1024], P('nodes'), may hold values from 0 to 1023, each once within a row
- enc_send_block: int32 [2048], P('nodes'), may hold values from 0 to 7
- enc_recv_block: int32 [2048], P('nodes'), may hold values from 0 to 7
- enc_offsets: int32 [2048, 2, 128], P('nodes'), may hold values from 0 to 127
- enc_classes: int32 [2048, 128], P('nodes'), may hold values from 0 to 7
- enc_live: int32 [128], P('nodes'), may hold values from 1 to 16, 1280 in all
- mesh_send_block: int32 [12288], P('nodes'), may hold values from 0 to 23
- mesh_recv_block: int32 [12288], P('nodes'), may hold values from 0 to 7
- mesh_offsets: int32 [12288, 2, 128], P('nodes'), may hold values from 0 to 127
- mesh_classes: int32 [12288, 128], P('nodes'), may hold values from 0 to 7
- mesh_live: int32 [128], P('nodes'), may hold values from 1 to 96, 7680 in all
- dec_send_block: int32 [3072], P('nodes'), may hold values from 0 to 7
- dec_recv_block: int32 [3072], P('nodes'), may hold values from 0 to 7
- dec_offsets: int32 [3072, 2, 128], P('nodes'), may hold values from 0 to 127
- dec_classes: int32 [3072, 128], P('nodes'), may hold values from 0 to 7
- dec_live: int32 [128], P('nodes'), may hold values from 1 to 24, 1920 in all
- class_gain: float32 [3, 8], replicated, may hold values from 0.25 to 2
- enc_weights: bfloat16 [3, 512, 512], P(None, None, 'feat'), may hold values from -0.25 to 0.25
- mesh_weights: bfloat16 [2, 3, 512, 512], P(None, None, None, 'feat'), may hold values from -0.25 to 0.25
- dec_weights: bfloat16 [3, 512, 512], P(None, None, 'feat'), may hold values from -0.25 to 0.25
- enc_bias: float32 [512], P('feat'), may hold values from -3 to 3
- enc_gain: float32 [512], P('feat'), may hold values from 0.25 to 1.75
- mesh_bias: float32 [2, 512], P(None, 'feat'), may hold values from -3 to 3
- mesh_gain: float32 [2, 512], P(None, 'feat'), may hold values from 0.25 to 1.75
- dec_bias: float32 [512], P('feat'), may hold values from -3 to 3
- dec_gain: float32 [512], P('feat'), may hold values from 0.25 to 1.75
Outputs:
- grid_out: bfloat16 [131072, 512], P('nodes', 'feat')
- mesh_final: bfloat16 [131072, 512], P('nodes', 'feat')
Inputs may be any that keep to these rules, and one draw needn't show every extreme that they name: Each row of grid_order lists each of 0..1023 once. The first enc_live[d] edge blocks of region d are live; the most is reached on some region. The first mesh_live[d] edge blocks of region d are live; the most is reached on some region. The first dec_live[d] edge blocks of region d are live; the most is reached on some region.
All inputs are finite; a program needn't handle non-finite values.
Results may differ from a plain program's by a relative error of at most 0.0085.
Values may be sent and summed in bfloat16 or wider, within the bound.
A program may use at most 64 MiB of HBM per device.

v0:
```python
import math

import jax
import jax.numpy as jnp
from jax import lax
from jax.sharding import PartitionSpec as P

D = 512
BLOCK = 128
ROUNDS = 2
NCLASS = 8


epsilon = 1e-05


def laid_out(parts, dim):
    parts = jnp.moveaxis(parts, 0, dim)
    shape = parts.shape
    return parts.reshape(*shape[:dim], shape[dim] * shape[dim + 1], *shape[dim + 2 :])


def copy_for_each(value, axis):
    copies = jnp.broadcast_to(value, (lax.axis_size(axis), *value.shape))
    return lax.all_to_all(copies, axis, split_axis=0, concat_axis=0, tiled=True)


def gather_directly(value, axis, dim):
    return laid_out(copy_for_each(value, axis), dim)


def total_of_pieces(value, axis):
    parts = lax.all_gather(value, axis)
    return parts.sum(axis=0)


def padded(value, sides, width):
    for axis, dim in sides:
        size, length = (lax.axis_size(axis), value.shape[dim])
        up = [(i, (i + 1) % size) for i in range(size)]
        down = [(j, i) for i, j in up]
        last = lax.slice_in_dim(value, length - width, length, axis=dim)
        leading = lax.slice_in_dim(value, 0, width, axis=dim)
        before = lax.ppermute(last, axis, up)
        after = lax.ppermute(leading, axis, down)
        value = jnp.concatenate([before, value, after], axis=dim)
    return value


def widened(inputs, matrices):
    piece = gather_directly(inputs, "feat", 1)
    return tuple(
        (jnp.dot(piece, matrix, preferred_element_type=jnp.float32) for matrix in matrices)
    )


def normalized(mixed, gain_vector):
    moments = (
        total_of_pieces(jnp.sum(mixed, axis=1), "feat"),
        total_of_pieces(jnp.sum(mixed * mixed, axis=1), "feat"),
    )
    average = moments[0] / D
    spread = moments[1] / D - average * average
    return (mixed - average[:, None]) * lax.rsqrt(spread[:, None] + epsilon) * gain_vector


def refreshed(gathered, matrix, gain_vector):
    (mixed,) = widened(gathered.astype(jnp.bfloat16), (matrix,))
    return normalized(mixed, gain_vector)


def edge_sum(
    sender,
    receiver,
    bias_row,
    class_row,
    send_ids,
    recv_ids,
    offset_pair,
    labels,
    live_count,
    block_count,
):
    columns_here = sender.shape[1]
    slots = send_ids.shape[0]
    blocks_turn = math.gcd(slots, 8)

    def turn(turn_index, running):
        opening = turn_index * blocks_turn
        sender_block = lax.dynamic_slice_in_dim(send_ids, opening, blocks_turn)
        taker_block = lax.dynamic_slice_in_dim(recv_ids, opening, blocks_turn)
        offsets_here = lax.dynamic_slice_in_dim(offset_pair, opening, blocks_turn)
        labels_here = lax.dynamic_slice_in_dim(labels, opening, blocks_turn)
        living = (opening + jnp.arange(blocks_turn, dtype=jnp.int32) < live_count).astype(
            jnp.float32
        )
        chosen = (labels_here[:, :, None] == jnp.arange(NCLASS, dtype=jnp.int32)).astype(
            jnp.float32
        )
        weight = jnp.sum(chosen * class_row, axis=-1) * living[:, None]
        sender_rows = sender_block[:, None] * BLOCK + offsets_here[:, 0, :]
        taker_rows = taker_block[:, None] * BLOCK + offsets_here[:, 1, :]
        summed = (
            sender[sender_rows].astype(jnp.float32)
            + receiver[taker_rows].astype(jnp.float32)
            + bias_row
        )
        message = (jax.nn.silu(summed) * weight[:, :, None]).astype(jnp.bfloat16)
        onehot = (offsets_here[:, 1, :, None] == jnp.arange(BLOCK, dtype=jnp.int32)).astype(
            jnp.bfloat16
        )
        block_sums = jnp.einsum("gei,ged->gid", onehot, message, preferred_element_type=jnp.float32)
        return running.at[taker_block].add(block_sums)

    zeroed = jnp.zeros((block_count, BLOCK, columns_here), jnp.float32)
    trip_count = (live_count + blocks_turn - 1) // blocks_turn
    running = lax.fori_loop(0, trip_count, turn, zeroed)
    return running.reshape(block_count * BLOCK, columns_here)


def local(
    grid_latent,
    mesh_latent,
    grid_order,
    enc_send_block,
    enc_recv_block,
    enc_offsets,
    enc_classes,
    enc_live,
    mesh_send_block,
    mesh_recv_block,
    mesh_offsets,
    mesh_classes,
    mesh_live,
    dec_send_block,
    dec_recv_block,
    dec_offsets,
    dec_classes,
    dec_live,
    class_gain,
    enc_weights,
    mesh_weights,
    dec_weights,
    enc_bias,
    enc_gain,
    mesh_bias,
    mesh_gain,
    dec_bias,
    dec_gain,
):
    routing = grid_order[0]
    grid_rows = grid_latent.shape[0]
    mesh_rows = mesh_latent.shape[0]
    arrived = lax.all_to_all(grid_latent[routing], "nodes", split_axis=0, concat_axis=0, tiled=True)
    send_away, take_away = widened(arrived, (enc_weights[0], dec_weights[1]))
    grid_send = send_away.astype(jnp.bfloat16)
    grid_take = take_away.astype(jnp.bfloat16)
    (mesh_take,) = widened(mesh_latent, (enc_weights[1],))
    enc_agg = edge_sum(
        grid_send,
        mesh_take.astype(jnp.bfloat16),
        enc_bias,
        class_gain[0],
        enc_send_block,
        enc_recv_block,
        enc_offsets,
        enc_classes,
        enc_live[0],
        mesh_rows // BLOCK,
    )
    mesh = (mesh_latent.astype(jnp.float32) + refreshed(enc_agg, enc_weights[2], enc_gain)).astype(
        jnp.bfloat16
    )
    for round_index in range(ROUNDS):
        weights = mesh_weights[round_index]
        sending, taking = widened(mesh, (weights[0], weights[1]))
        sending = sending.astype(jnp.bfloat16)
        nearby = padded(sending, (("nodes", 0),), sending.shape[0])
        mesh_agg = edge_sum(
            nearby,
            taking.astype(jnp.bfloat16),
            mesh_bias[round_index],
            class_gain[1],
            mesh_send_block,
            mesh_recv_block,
            mesh_offsets,
            mesh_classes,
            mesh_live[0],
            mesh_rows // BLOCK,
        )
        mesh = (
            mesh.astype(jnp.float32) + refreshed(mesh_agg, weights[2], mesh_gain[round_index])
        ).astype(jnp.bfloat16)
    (dec_send,) = widened(mesh, (dec_weights[0],))
    dec_agg = edge_sum(
        dec_send.astype(jnp.bfloat16),
        grid_take,
        dec_bias,
        class_gain[2],
        dec_send_block,
        dec_recv_block,
        dec_offsets,
        dec_classes,
        dec_live[0],
        grid_rows // BLOCK,
    )
    update = refreshed(dec_agg, dec_weights[2], dec_gain).astype(jnp.bfloat16)
    returned = lax.all_to_all(update, "nodes", split_axis=0, concat_axis=0, tiled=True)
    placed = jnp.zeros_like(returned).at[routing].set(returned)
    grid_out = (grid_latent.astype(jnp.float32) + placed.astype(jnp.float32)).astype(jnp.bfloat16)
    return (grid_out, mesh)


def solution(mesh):
    in_specs = (
        P("nodes", "feat"),
        P("nodes", "feat"),
        P("nodes", None),
        P("nodes"),
        P("nodes"),
        P("nodes", None, None),
        P("nodes", None),
        P("nodes"),
        P("nodes"),
        P("nodes"),
        P("nodes", None, None),
        P("nodes", None),
        P("nodes"),
        P("nodes"),
        P("nodes"),
        P("nodes", None, None),
        P("nodes", None),
        P("nodes"),
        P(),
        P(None, None, "feat"),
        P(None, None, None, "feat"),
        P(None, None, "feat"),
        P("feat"),
        P("feat"),
        P(None, "feat"),
        P(None, "feat"),
        P("feat"),
        P("feat"),
    )
    out_specs = (P("nodes", "feat"), P("nodes", "feat"))
    return jax.shard_map(local, mesh=mesh, in_specs=in_specs, out_specs=out_specs, check_vma=False)
```

profile of v0, /device:TPU:2, one launch (start us, length us, event | category | flops | bytes accessed | tf_op | source)
XLA Modules:
  0.0 630.0 jit_solution(16636257436666600525)
XLA Ops:
  6.7 5.0 gather_fusion.8
  11.7 15.4 %all-to-all-start = ((bf16[128,8,256]{2,1,0:T(8,128)(2,1)}), bf16[128,8,256]{2,1,0:T(8,128)(2,1)S(1)}, u32[]{:S(2)}, u32[]{:S(2)}) async-start(bf16[128,8,256]{2,1,0:T(8,128)(2,1)} %bitcast.34), calls=%async_computation | async-start | bytes 1048576 | tf_op jit(solution)/shard_map/all_to_all | solution.py:154
  29.2 18.7 %all-to-all-done = bf16[128,8,256]{2,1,0:T(8,128)(2,1)S(1)} async-done(((bf16[128,8,256]{2,1,0:T(8,128)(2,1)}), bf16[128,8,256]{2,1,0:T(8,128)(2,1)S(1)}, u32[]{:S(2)}, u32[]{:S(2)}) %all-to-all-start) | async-done | bytes 524320 | tf_op jit(solution)/shard_map/all_to_all | solution.py:154
  48.3 4.6 all_to_all.69
  54.9 21.9 %while.40 = (s32[]{:T(128)}, f32[8,128,256]{2,1,0:T(8,128)S(1)}, s32[]{:T(128)}, s32[16]{0:T(128)S(1)}, s32[16,2,128]{2,1,0:T(2,128)S(1)}, /*index=5*/s32[16]{0:...) while((s32[]{:T(128)}, f32[8,128,256]{2,1,0:T(8,128)S(1)}, ...), condition=%wide.region_3.4_spmd, body=%wide.region_0.3_spmd.sunk | while | flops 70158408 | bytes 9512527 | solution.py:117
  77.2 4.6 all_to_all.70
  87.4 4.6 all_to_all.71
  98.4 9.1 %collective-permute-done.1 = bf16[1024,256]{1,0:T(8,128)(2,1)S(1)} collective-permute-done((bf16[1024,256]{1,0:T(8,128)(2,1)S(1)}, bf16[1024,256]{1,0:T(8,128)(2,1)S(1)}, u32[]{:S(2)}, u32[]{:S(2)}) %collective-permute-start.1) | collective-permute-done | bytes 524320 | tf_op jit(solution)/shard_map/ppermute | solution.py:45
  113.4 176.2 %while.41 = (s32[]{:T(128)}, f32[8,128,256]{2,1,0:T(8,128)}, s32[]{:T(128)}, s32[96]{0:T(128)S(1)}, s32[96,2,128]{2,0,1:T(8,128)S(1)}, /*index=5*/s32[96]{0:T(12...) while((s32[]{:T(128)}, f32[8,128,256]{2,1,0:T(8,128)}, ...), condition=%wide.region_11.12_spmd, body=%wide.region_8.11_spmd.sunk | while | flops 70158408 | bytes 17893008 | solution.py:117
  291.3 4.6 all_to_all.72
  301.5 4.6 all_to_all.73
  312.6 9.1 %collective-permute-done.3 = bf16[1024,256]{1,0:T(8,128)(2,1)S(1)} collective-permute-done((bf16[1024,256]{1,0:T(8,128)(2,1)S(1)}, bf16[1024,256]{1,0:T(8,128)(2,1)S(1)}, u32[]{:S(2)}, u32[]{:S(2)}) %collective-permute-start.3) | collective-permute-done | bytes 524320 | tf_op jit(solution)/shard_map/ppermute | solution.py:45
  325.0 202.6 %while.42 = (s32[]{:T(128)}, f32[8,128,256]{2,1,0:T(8,128)}, s32[]{:T(128)}, s32[96]{0:T(128)S(1)}, s32[96,2,128]{2,0,1:T(8,128)S(1)}, /*index=5*/s32[96]{0:T(12...) while((s32[]{:T(128)}, f32[8,128,256]{2,1,0:T(8,128)}, ...), condition=%wide.region_19.20_spmd, body=%wide.region_16.19_spmd.sunk | while | flops 70158408 | bytes 9504343 | solution.py:117
  330.6 5.0 gather_fusion.5
  347.5 5.0 gather_fusion.5
  364.4 5.0 gather_fusion.5
  381.3 5.0 gather_fusion.5
  398.2 5.0 gather_fusion.5
  415.1 5.0 gather_fusion.5
  431.9 5.0 gather_fusion.5
  448.8 5.0 gather_fusion.5
  465.7 5.0 gather_fusion.5
  482.6 5.0 gather_fusion.5
  499.5 5.0 gather_fusion.5
  516.3 5.0 gather_fusion.5
  529.3 4.6 all_to_all.74
  539.5 4.6 all_to_all.75
  545.6 12.6 %while.43 = (s32[]{:T(128)}, f32[8,128,256]{2,1,0:T(8,128)S(1)}, s32[]{:T(128)}, s32[24]{0:T(128)S(1)}, s32[24,2,128]{2,1,0:T(2,128)}, /*index=5*/s32[24]{0:T(12...) while((s32[]{:T(128)}, f32[8,128,256]{2,1,0:T(8,128)S(1)}, ...), condition=%wide.region_27.28_spmd, body=%wide.region_24.27_spmd.sunk | while | flops 70158408 | bytes 9512527 | solution.py:117
  558.7 4.6 all_to_all.76
  569.9 33.5 %all-to-all-start.10 = ((bf16[128,8,256]{2,1,0:T(8,128)(2,1)}), bf16[128,8,256]{2,1,0:T(8,128)(2,1)S(1)}, u32[]{:S(2)}, u32[]{:S(2)}) async-start(bf16[128,8,256]{2,1,0:T(8,128)(2,1)} %fusion.30), calls=%async_computation.10 | async-start | bytes 1048576 | tf_op jit(solution)/shard_map/all_to_all | solution.py:208
  604.5 19.5 %all-to-all-done.10 = bf16[128,8,256]{2,1,0:T(8,128)(2,1)S(1)} async-done(((bf16[128,8,256]{2,1,0:T(8,128)(2,1)}), bf16[128,8,256]{2,1,0:T(8,128)(2,1)S(1)}, u32[]{:S(2)}, u32[]{:S(2)}) %all-to-all-start.10) | async-done | bytes 524320 | tf_op jit(solution)/shard_map/all_to_all | solution.py:208
  624.0 5.1 scatter_custom_fusion.4
  (506 shorter events, 413.4 us)
Async XLA Ops:
  1.9 4.7 copy-start.23
  1.9 4.8 copy-start.2
  3.0 8.6 %all-to-all-start.2 = ((bf16[2,1024,256]{1,2,0:T(8,128)(2,1)}), bf16[2,1024,256]{1,2,0:T(8,128)(2,1)S(1)}, u32[]{:S(2)}, u32[]{:S(2)}) async-start(bf16[2,1024,256]{1,2,0:T(8,128)(2,1)} %broadcast_in_dim.51), calls=%async_computation.2 | async-start | bytes 2097152 | tf_op jit(solution)/shard_map/all_to_all | solution.py:25
  6.7 21.1 %copy-start.26 = (f32[3,8]{1,0:T(4,128)S(1)}, f32[3,8]{1,0:T(4,128)}, u32[]{:S(2)}) copy-start(f32[3,8]{1,0:T(4,128)} %param.54) | copy-start | bytes 292
  11.7 36.2 %all-to-all-start = ((bf16[128,8,256]{2,1,0:T(8,128)(2,1)}), bf16[128,8,256]{2,1,0:T(8,128)(2,1)S(1)}, u32[]{:S(2)}, u32[]{:S(2)}) async-start(bf16[128,8,256]{2,1,0:T(8,128)(2,1)} %bitcast.34), calls=%async_computation | async-start | bytes 1048576 | tf_op jit(solution)/shard_map/all_to_all | solution.py:154
  52.8 1.9 copy-start.12
  52.8 2.0 copy-start.14
  52.8 2.0 copy-start.16
  52.9 2.0 copy-start.19
  52.9 2.0 copy-start.20
  52.9 2.0 copy-start.29
  81.8 5.2 copy-start.5
  81.8 5.2 copy-start.27
  87.2 4.7 copy-start.8
  92.0 3.6 copy-start.24
  92.0 4.9 copy-start.15
  92.0 5.0 copy-start.25
  93.4 14.0 %collective-permute-start.1 = (bf16[1024,256]{1,0:T(8,128)(2,1)S(1)}, bf16[1024,256]{1,0:T(8,128)(2,1)S(1)}, u32[]{:S(2)}, u32[]{:S(2)}) collective-permute-start(bf16[1024,256]{1,0:T(8,128)(2,1)S(1)} %convolution_convert_fusion.5), channel_id=1, source_target_pairs={{2,0},{4,2},{6,4},{8,6},{10,8},{12,10},{14,12},{16,14},{18,16},{20... | collective-permute-start | bytes 1572872 | tf_op jit(solution)/shard_map/ppermute | solution.py:45
  95.3 15.9 %collective-permute-start = (bf16[1024,256]{1,0:T(8,128)(2,1)S(1)}, bf16[1024,256]{1,0:T(8,128)(2,1)}, u32[]{:S(2)}, u32[]{:S(2)}) collective-permute-start(bf16[1024,256]{1,0:T(8,128)(2,1)S(1)} %convolution_convert_fusion.5), channel_id=1, source_target_pairs={{0,2},{2,4},{4,6},{6,8},{8,10},{10,12},{12,14},{14,16},{16,18},{18... | collective-permute-start | bytes 1572872 | tf_op jit(solution)/shard_map/ppermute | solution.py:44
  98.4 15.0 %copy-start.17 = (s32[96]{0:T(128)S(1)}, s32[96]{0:T(128)}, u32[]{:S(2)}) copy-start(s32[96]{0:T(128)} %param.45) | copy-start | bytes 1156
  98.4 15.0 %copy-start.18 = (s32[96]{0:T(128)S(1)}, s32[96]{0:T(128)}, u32[]{:S(2)}) copy-start(s32[96]{0:T(128)} %param.44) | copy-start | bytes 1156
  295.8 5.2 copy-start.9
  301.3 4.7 copy-start.10
  306.0 3.6 copy-start.13
  307.6 14.0 %collective-permute-start.3 = (bf16[1024,256]{1,0:T(8,128)(2,1)S(1)}, bf16[1024,256]{1,0:T(8,128)(2,1)S(1)}, u32[]{:S(2)}, u32[]{:S(2)}) collective-permute-start(bf16[1024,256]{1,0:T(8,128)(2,1)S(1)} %convolution_convert_fusion.3), channel_id=1, source_target_pairs={{2,0},{4,2},{6,4},{8,6},{10,8},{12,10},{14,12},{16,14},{18,16},{20... | collective-permute-start | bytes 1572872 | tf_op jit(solution)/shard_map/ppermute | solution.py:45
  307.8 16.0 %collective-permute-start.2 = (bf16[1024,256]{1,0:T(8,128)(2,1)S(1)}, bf16[1024,256]{1,0:T(8,128)(2,1)S(1)}, u32[]{:S(2)}, u32[]{:S(2)}) collective-permute-start(bf16[1024,256]{1,0:T(8,128)(2,1)S(1)} %convolution_convert_fusion.3), channel_id=1, source_target_pairs={{0,2},{2,4},{4,6},{6,8},{8,10},{10,12},{12,14},{14,16},{16,18},{18... | collective-permute-start | bytes 1572872 | tf_op jit(solution)/shard_map/ppermute | solution.py:44
  533.8 5.2 copy-start.11
  539.3 4.7 copy-start.6
  563.2 5.6 copy-start.28
  564.9 38.6 %copy-start.7 = (bf16[1024,256]{0,1:T(8,128)(2,1)S(1)}, bf16[1024,256]{0,1:T(8,128)(2,1)}, u32[]{:S(2)}) copy-start(bf16[1024,256]{0,1:T(8,128)(2,1)} %copy-done.6) | copy-start | bytes 1572868
  569.9 59.1 %copy-start.3 = (bf16[1024,256]{1,0:T(8,128)(2,1)S(1)}, bf16[1024,256]{1,0:T(8,128)(2,1)}, u32[]{:S(2)}) copy-start(bf16[1024,256]{1,0:T(8,128)(2,1)} %param.36) | copy-start | bytes 1572868
  569.9 54.0 %all-to-all-start.10 = ((bf16[128,8,256]{2,1,0:T(8,128)(2,1)}), bf16[128,8,256]{2,1,0:T(8,128)(2,1)S(1)}, u32[]{:S(2)}, u32[]{:S(2)}) async-start(bf16[128,8,256]{2,1,0:T(8,128)(2,1)} %fusion.30), calls=%async_computation.10 | async-start | bytes 1048576 | tf_op jit(solution)/shard_map/all_to_all | solution.py:208
  (28 other events, 36.4 us)
where the time goes:
time: 636 us; the launch traced here: 630 us
  local copies, waits for them, and re-layouts  274 us (43%)
  other arithmetic  125 us (20%)
  waiting for transfers between devices  62.1 us (10%)
  starting transfers between devices  56.8 us (9%)
  matrix products  56.2 us (9%)
  blocking collectives  51.3 us (8%)
    gather x27, local copies, waits for them, and re-layouts, turn(): sender[sender_rows].astype(jnp.float32)  119 us
    gather x27, local copies, waits for them, and re-layouts, turn(): receiver[taker_rows].astype(jnp.float32)  106 us
    scatter-add x27, other arithmetic, turn(): return running.at[taker_block].add(block_sums)  76.8 us
    dot_general x27, matrix products, turn(): jnp.einsum('gei,ged->gid', onehot, message, preferred_element_type=jnp.fl...  38 us
    all_to_all x8, blocking collectives, copy_for_each(): return lax.all_to_all(copies, axis, split_axis=0, concat_axis=0, tiled=True)  36.6 us
    all_to_all x1, starting transfers between devices, local(): lax.all_to_all(update, 'nodes', split_axis=0, concat_axis=0, tiled=True)  33.5 us
    all_to_all x1, waiting for transfers between devices, local(): lax.all_to_all(update, 'nodes', split_axis=0, concat_axis=0, tiled=True)  19.5 us
    all_to_all x1, waiting for transfers between devices, local(): lax.all_to_all(grid_latent[routing], 'nodes', split_axis=0, concat_axis=0...  18.7 us
  transfers between devices with their start and end apart: 7, of which 6 were waited for; matrix products, arithmetic and copies ran while one was open for 2% of the time, Pallas kernels for 0%

commit v1 on v0

v1 whole, which is shorter than its diff:
```python
import functools

import jax
import jax.numpy as jnp
from jax import lax
from jax.experimental import pallas as pl
from jax.experimental.pallas import tpu as pltpu
from jax.sharding import PartitionSpec as P

D = 512
BLOCK = 128
ROUNDS = 2
NCLASS = 8
EPS = 1e-05
F32 = jnp.float32
BF16 = jnp.bfloat16

VMEM = pl.BlockSpec(memory_space=pltpu.VMEM)
SMEM = pl.BlockSpec(memory_space=pltpu.SMEM)


def call(kernel, ins, outs, scratch=(), flops=1 << 28, **params):
    return pl.pallas_call(
        kernel,
        in_specs=ins,
        out_specs=[VMEM] * len(outs) if isinstance(outs, (list, tuple)) else VMEM,
        out_shape=outs,
        scratch_shapes=list(scratch),
        cost_estimate=pl.CostEstimate(flops=flops, bytes_accessed=1 << 20, transcendentals=0),
        compiler_params=pltpu.CompilerParams(**params),
    )


def dot(a, b, dims=((1,), (0,))):
    return lax.dot_general(a, b, (dims, ((), ())), preferred_element_type=F32)


def edge_kernel(unroll, send_ids, recv_ids, live, gains, offsets, labels, bias, sender, receiver, out, total, weights, shift):
    slots = labels.shape[0]
    width = bias.shape[0]
    blocks = total.shape[0]
    chosen = labels[...]
    weight = jnp.zeros((slots, BLOCK), F32)
    for c in range(NCLASS):
        weight = jnp.where(chosen == c, gains[c], weight)
    alive = lax.broadcasted_iota(jnp.int32, (slots, BLOCK), 0) < live[0]
    weights[...] = jnp.where(alive, weight, 0.0)
    shift[...] = jnp.broadcast_to(bias[...] * 0.5, (width, BLOCK))
    total[...] = jnp.zeros_like(total)
    rows = lax.broadcasted_iota(jnp.int32, (BLOCK, BLOCK), 0)

    def turn(t, carry):
        sums = []
        for u in range(unroll):
            k = t * unroll + u
            pair = offsets[k]
            from_hot = jnp.where(rows == pair[0:1, :], 0.5, 0.0).astype(BF16)
            to_hot = jnp.where(rows == pair[1:2, :], 0.5, 0.0).astype(BF16)
            hot = jnp.concatenate([from_hot, to_hot], axis=0)
            both = jnp.concatenate([sender[send_ids[k]], receiver[recv_ids[k]]], axis=1)
            half = dot(both, hot) + shift[...]
            message = (half * (1.0 + jnp.tanh(half))) * weights[pl.ds(k, 1), :]
            sums.append(dot(message.astype(BF16), to_hot, ((1,), (1,))))
        for u in range(unroll):
            taker = recv_ids[t * unroll + u]
            total[taker] = total[taker] + sums[u]
        return carry

    lax.fori_loop(0, (live[0] + unroll - 1) // unroll, turn, 0)
    for b in range(blocks):
        out[b * BLOCK : (b + 1) * BLOCK, :] = (total[b] * 2.0).T.astype(BF16)


def edge_sum(sender, receiver, bias, gains, send_ids, recv_ids, offsets, labels, live, unroll=4):
    slots = labels.shape[0]
    blocks, width, _ = receiver.shape
    return call(
        functools.partial(edge_kernel, unroll),
        [SMEM] * 4 + [VMEM] * 5,
        jax.ShapeDtypeStruct((blocks * BLOCK, width), BF16),
        [
            pltpu.VMEM((blocks, width, BLOCK), F32),
            pltpu.VMEM((slots, BLOCK), F32),
            pltpu.VMEM((width, BLOCK), F32),
        ],
    )(send_ids, recv_ids, live, gains, offsets, labels, bias[:, None], sender, receiver)


def halves(matrix, feat):
    half = matrix.shape[0] // 2
    own = matrix[pl.ds(pl.multiple_of(feat * half, half), half), :]
    peer = matrix[pl.ds(pl.multiple_of((1 - feat) * half, half), half), :]
    return own, peer


def project_kernel(count, *refs):
    own, peer = refs[:2]
    matrices = refs[2 : 2 + count]
    outs = refs[2 + count :]
    feat = lax.axis_index("feat")
    blocks = outs[0].shape[0]

    def step(b, carry):
        rows = pl.ds(pl.multiple_of(b * BLOCK, BLOCK), BLOCK)
        a, p = own[rows, :], peer[rows, :]
        for matrix, out in zip(matrices, outs):
            m, n = halves(matrix, feat)
            out[b] = (dot(m, a, ((0,), (1,))) + dot(n, p, ((0,), (1,)))).astype(BF16)
        return carry

    lax.fori_loop(0, blocks, step, 0)


def project(own, peer, matrices):
    blocks = own.shape[0] // BLOCK
    return call(
        functools.partial(project_kernel, len(matrices)),
        [VMEM] * (2 + len(matrices)),
        [jax.ShapeDtypeStruct((blocks, m.shape[1], BLOCK), BF16) for m in matrices],
    )(own, peer, *matrices)


def normed(mixed_own, mixed_peer, gain_own, gain_peer):
    total = jnp.sum(mixed_own, axis=1, keepdims=True) + jnp.sum(mixed_peer, axis=1, keepdims=True)
    square = jnp.sum(mixed_own * mixed_own, axis=1, keepdims=True) + jnp.sum(
        mixed_peer * mixed_peer, axis=1, keepdims=True
    )
    average = total * (1.0 / D)
    spread = square * (1.0 / D) - average * average
    scale = lax.rsqrt(spread + EPS)
    mine = (mixed_own - average) * scale * gain_own
    if gain_peer is None:
        return mine, None
    return mine, (mixed_peer - average) * scale * gain_peer


def refresh_kernel(count, agg_own, agg_peer, w_own, w_peer, gain_own, gain_peer, mesh_own, mesh_peer, *refs):
    matrices = refs[:count]
    new_own, new_peer = refs[count : count + 2]
    outs = refs[count + 2 :]
    feat = lax.axis_index("feat")
    blocks = outs[0].shape[0]

    def step(b, carry):
        rows = pl.ds(pl.multiple_of(b * BLOCK, BLOCK), BLOCK)
        a, p = agg_own[rows, :], agg_peer[rows, :]
        m, n = halves(w_own, feat)
        mixed_own = dot(a, m) + dot(p, n)
        m, n = halves(w_peer, feat)
        mixed_peer = dot(a, m) + dot(p, n)
        own, peer = normed(mixed_own, mixed_peer, gain_own[...], gain_peer[...])
        own = (mesh_own[rows, :].astype(F32) + own).astype(BF16)
        peer = (mesh_peer[rows, :].astype(F32) + peer).astype(BF16)
        new_own[rows, :] = own
        new_peer[rows, :] = peer
        for matrix, out in zip(matrices, outs):
            m, n = halves(matrix, feat)
            out[b] = (dot(m, own, ((0,), (1,))) + dot(n, peer, ((0,), (1,)))).astype(BF16)
        return carry

    lax.fori_loop(0, blocks, step, 0)


def refresh(agg_own, agg_peer, w_own, w_peer, gain_own, gain_peer, mesh_own, mesh_peer, matrices):
    blocks = agg_own.shape[0] // BLOCK
    shape = jax.ShapeDtypeStruct(agg_own.shape, BF16)
    return call(
        functools.partial(refresh_kernel, len(matrices)),
        [VMEM] * (8 + len(matrices)),
        [shape, shape] + [jax.ShapeDtypeStruct((blocks, m.shape[1], BLOCK), BF16) for m in matrices],
    )(agg_own, agg_peer, w_own, w_peer, gain_own, gain_peer, mesh_own, mesh_peer, *matrices)


def update_kernel(agg_own, agg_peer, w_own, w_peer, gain_own, out):
    feat = lax.axis_index("feat")

    def step(b, carry):
        rows = pl.ds(pl.multiple_of(b * BLOCK, BLOCK), BLOCK)
        a, p = agg_own[rows, :], agg_peer[rows, :]
        m, n = halves(w_own, feat)
        mixed_own = dot(a, m) + dot(p, n)
        m, n = halves(w_peer, feat)
        mixed_peer = dot(a, m) + dot(p, n)
        own, _ = normed(mixed_own, mixed_peer, gain_own[...], None)
        out[rows, :] = own.astype(BF16)
        return carry

    lax.fori_loop(0, agg_own.shape[0] // BLOCK, step, 0)


def update_of(agg_own, agg_peer, w_own, w_peer, gain_own):
    return call(update_kernel, [VMEM] * 5, jax.ShapeDtypeStruct(agg_own.shape, BF16))(
        agg_own, agg_peer, w_own, w_peer, gain_own
    )


def pick_kernel(order, grid, out):
    rows = grid.shape[0]

    def step(b, carry):
        here = pl.ds(pl.multiple_of(b * BLOCK, BLOCK), BLOCK)
        spot = lax.broadcasted_iota(jnp.int32, (BLOCK, rows), 1)
        hot = jnp.where(spot == order[here, :], 1.0, 0.0).astype(BF16)
        out[here, :] = dot(hot, grid[...]).astype(BF16)
        return carry

    lax.fori_loop(0, rows // BLOCK, step, 0)


def pick(order, grid):
    return call(pick_kernel, [VMEM] * 2, jax.ShapeDtypeStruct(grid.shape, BF16))(order[:, None], grid)


def place_kernel(order, returned, grid, out):
    rows = grid.shape[0]

    def step(b, carry):
        start = pl.multiple_of(b * BLOCK, BLOCK)
        here = pl.ds(start, BLOCK)
        spot = lax.broadcasted_iota(jnp.int32, (BLOCK, rows), 0) + start
        hot = jnp.where(spot == order[...], 1.0, 0.0).astype(BF16)
        out[here, :] = (grid[here, :].astype(F32) + dot(hot, returned[...])).astype(BF16)
        return carry

    lax.fori_loop(0, rows // BLOCK, step, 0)


def place(order, returned, grid):
    return call(place_kernel, [VMEM] * 3, jax.ShapeDtypeStruct(grid.shape, BF16))(order[None, :], returned, grid)


def swapped(value):
    return lax.ppermute(value, "feat", [(0, 1), (1, 0)])


def neighbours(value):
    size = lax.axis_size("nodes")
    up = [(i, (i + 1) % size) for i in range(size)]
    down = [(j, i) for i, j in up]
    before = lax.ppermute(value, "nodes", up)
    after = lax.ppermute(value, "nodes", down)
    return jnp.concatenate([before, value, after], axis=0)


def local(
    grid_latent,
    mesh_latent,
    grid_order,
    enc_send_block,
    enc_recv_block,
    enc_offsets,
    enc_classes,
    enc_live,
    mesh_send_block,
    mesh_recv_block,
    mesh_offsets,
    mesh_classes,
    mesh_live,
    dec_send_block,
    dec_recv_block,
    dec_offsets,
    dec_classes,
    dec_live,
    class_gain,
    enc_weights,
    mesh_weights,
    dec_weights,
    enc_bias,
    enc_gain,
    mesh_bias,
    mesh_gain,
    dec_bias,
    dec_gain,
):
    order = grid_order[0]
    arrived = lax.all_to_all(pick(order, grid_latent), "nodes", split_axis=0, concat_axis=0, tiled=True)
    outer = jnp.stack([enc_weights[2], mesh_weights[0, 2], mesh_weights[1, 2], dec_weights[2]])
    outer_peer = swapped(outer)
    gains = jnp.stack([enc_gain, mesh_gain[0], mesh_gain[1], dec_gain])
    gains_peer = swapped(gains)
    mesh_own = mesh_latent
    mesh_peer = swapped(mesh_latent)
    (mesh_take,) = project(mesh_own, mesh_peer, (enc_weights[1],))
    grid_send, grid_take = project(arrived, swapped(arrived), (enc_weights[0], dec_weights[1]))
    agg = edge_sum(
        grid_send, mesh_take, enc_bias, class_gain[0],
        enc_send_block, enc_recv_block, enc_offsets, enc_classes, enc_live,
    )
    following = [(mesh_weights[0, 0], mesh_weights[0, 1]), (mesh_weights[1, 0], mesh_weights[1, 1]), (dec_weights[0],)]
    for stage in range(ROUNDS + 1):
        mesh_own, mesh_peer, *sides = refresh(
            agg, swapped(agg), outer[stage], outer_peer[stage],
            gains[stage][None, :], gains_peer[stage][None, :], mesh_own, mesh_peer, following[stage],
        )
        if stage < ROUNDS:
            sending, taking = sides
            agg = edge_sum(
                neighbours(sending), taking, mesh_bias[stage], class_gain[1],
                mesh_send_block, mesh_recv_block, mesh_offsets, mesh_classes, mesh_live,
            )
    (dec_send,) = sides
    agg = edge_sum(
        dec_send, grid_take, dec_bias, class_gain[2],
        dec_send_block, dec_recv_block, dec_offsets, dec_classes, dec_live,
    )
    update = update_of(agg, swapped(agg), outer[ROUNDS + 1], outer_peer[ROUNDS + 1], gains[ROUNDS + 1][None, :])
    returned = lax.all_to_all(update, "nodes", split_axis=0, concat_axis=0, tiled=True)
    return (place(order, returned, grid_latent), mesh_own)


def solution(mesh):
    in_specs = (
        P("nodes", "feat"),
        P("nodes", "feat"),
        P("nodes", None),
        P("nodes"),
        P("nodes"),
        P("nodes", None, None),
        P("nodes", None),
        P("nodes"),
        P("nodes"),
        P("nodes"),
        P("nodes", None, None),
        P("nodes", None),
        P("nodes"),
        P("nodes"),
        P("nodes"),
        P("nodes", None, None),
        P("nodes", None),
        P("nodes"),
        P(),
        P(None, None, "feat"),
        P(None, None, None, "feat"),
        P(None, None, "feat"),
        P("feat"),
        P("feat"),
        P(None, "feat"),
        P(None, "feat"),
        P("feat"),
        P("feat"),
    )
    out_specs = (P("nodes", "feat"), P("nodes", "feat"))
    return jax.shard_map(local, mesh=mesh, in_specs=in_specs, out_specs=out_specs, check_vma=False)
```

time: 636 us -> 236 us (0.37)
  local copies, waits for them, and re-layouts: 274 us -> 15.6 us
  other arithmetic: 125 us -> 5.9 us
  Pallas kernels: 0 us -> 71.7 us
  matrix products: 56.2 us -> 0 us
  starting transfers between devices: 56.8 us -> 25.1 us
  waiting for transfers between devices: 62.1 us -> 54.3 us
    gather x55 -> x0, local copies, waits for them, and re-layouts: 230 us -> none  [the longest x27 119 us: turn(): sender[sender_rows].astype(jnp.float32)]
    scatter-add x27 -> x0, other arithmetic: 76.8 us -> none  [turn(): return running.at[taker_block].add(block_sums)]
    pallas_call x0 -> x12, Pallas kernels: none -> 71.7 us  [the longest x4 25.8 us: edge_sum(): call(functools.partial(edge_kernel, unroll), [SMEM] * 4 + [VMEM] * 5, jax...]
    dot_general x39 -> x0, matrix products: 56.2 us -> none  [the longest x27 38 us: turn(): jnp.einsum('gei,ged->gid', onehot, message, preferred_element_type=jnp.fl...]
    all_to_all x3 -> x1, starting transfers between devices: 52.5 us -> 15.6 us  [local(): lax.all_to_all(pick(order, grid_latent), 'nodes', split_axis=0, concat_ax...]
    all_to_all x3 -> x1, waiting for transfers between devices: 38.2 us -> 15.5 us  [local(): lax.all_to_all(pick(order, grid_latent), 'nodes', split_axis=0, concat_ax...]
    convert_element_type x35 -> x0, other arithmetic: 21.8 us -> none  [the longest x27 17.5 us: turn(): (opening + jnp.arange(blocks_turn, dtype=jnp.int32) < live_count).astype(...]
    all_to_all x8 -> x1, blocking collectives: 36.6 us -> 56.8 us  [local(): lax.all_to_all(update, 'nodes', split_axis=0, concat_axis=0, tiled=True)]
  transfers between devices with their start and end apart: 7 -> 13, of which waited for: 6 -> 9; matrix products, arithmetic and copies ran while one was open for 2% -> 4% of each run, Pallas kernels for 0% -> 5%
where the time goes in v1:
time: 236 us; the launch traced here: 232 us
  Pallas kernels  71.7 us (30%)
  blocking collectives  56.8 us (24%)
  waiting for transfers between devices  54.3 us (23%)
  starting transfers between devices  25.1 us (11%)
  local copies, waits for them, and re-layouts  15.6 us (7%)
  other arithmetic  5.9 us (2%)
  between operations  2.68 us (1%)
    all_to_all x1, blocking collectives, local(): lax.all_to_all(update, 'nodes', split_axis=0, concat_axis=0, tiled=True)  56.8 us
    pallas_call x4, Pallas kernels, edge_sum(): call(functools.partial(edge_kernel, unroll), [SMEM] * 4 + [VMEM] * 5, jax...  25.8 us
    pallas_call x3, Pallas kernels, refresh(): call(functools.partial(refresh_kernel, len(matrices)), [VMEM] * (8 + len(...  23.4 us
    ppermute x2, waiting for transfers between devices, neighbours(): before = lax.ppermute(value, 'nodes', up)  22.3 us
    all_to_all x1, starting transfers between devices, local(): lax.all_to_all(pick(order, grid_latent), 'nodes', split_axis=0, concat_ax...  15.6 us
    all_to_all x1, waiting for transfers between devices, local(): lax.all_to_all(pick(order, grid_latent), 'nodes', split_axis=0, concat_ax...  15.5 us
    ppermute x2, waiting for transfers between devices, neighbours(): after = lax.ppermute(value, 'nodes', down)  10.7 us
    pallas_call x2, Pallas kernels, project(): call(functools.partial(project_kernel, len(matrices)), [VMEM] * (2 + len(...  9.42 us
  transfers between devices with their start and end apart: 13, of which 9 were waited for; matrix products, arithmetic and copies ran while one was open for 4% of the time, Pallas kernels for 5%

profile of v1, /device:TPU:2, one launch (start us, length us, event | category | flops | bytes accessed | tf_op | source)
XLA Modules:
  0.0 232.1 jit_solution(1760092723682038288)
XLA Ops:
  0.6 1.8 copy.30.order
  2.4 4.2 %shard_map.275 = bf16[1024,256]{1,0:T(8,128)(2,1)} custom-call(s32[1024,1]{1,0:T(8,128)} %copy.30.order, bf16[1024,256]{1,0:T(8,128)(2,1)} %grid.3), custom_call_target="tpu_custom_call" | custom-call | flops 268435456 | bytes 1048576 | tf_op jit(solution)/shard_map/pallas_call | solution.py:211
  6.6 15.6 %all-to-all-start = ((bf16[128,8,256]{2,1,0:T(8,128)(2,1)}), bf16[128,8,256]{2,1,0:T(8,128)(2,1)S(1)}, u32[]{:S(2)}, u32[]{:S(2)}) async-start(bf16[128,8,256]{2,1,0:T(8,128)(2,1)} %bitcast.57), calls=%async_computation | async-start | bytes 1048576 | tf_op jit(solution)/shard_map/all_to_all | solution.py:276
  23.1 0.9 slice_bitcast_fusion.21
  24.0 1.2 slice_bitcast_fusion.12
  25.2 1.1 pad_maximum_fusion.2
  26.8 15.5 %all-to-all-done = bf16[128,8,256]{2,1,0:T(8,128)(2,1)S(1)} async-done(((bf16[128,8,256]{2,1,0:T(8,128)(2,1)}), bf16[128,8,256]{2,1,0:T(8,128)(2,1)S(1)}, u32[]{:S(2)}, u32[]{:S(2)}) %all-to-all-start) | async-done | bytes 524320 | tf_op jit(solution)/shard_map/all_to_all | solution.py:276
  45.2 4.3 %shard_map.277.receiver = bf16[8,256,128]{2,1,0:T(8,128)(2,1)} custom-call(bf16[1024,256]{1,0:T(8,128)(2,1)} %mesh_own.1, bf16[1024,256]{1,0:T(8,128)(2,1)} %copy-done.2, bf16[512,256]{1,0:T(8,128)(2,1)} %get-tuple-element.45.refs_2_), custom_call_target="tpu_custom_call" | custom-call | flops 268435456 | bytes 1048576 | tf_op jit(solution)/shard_map/pallas_call | solution.py:116
  50.3 5.2 %shard_map.276 = (bf16[8,256,128]{2,1,0:T(8,128)(2,1)}, bf16[8,256,128]{2,1,0:T(8,128)(2,1)}) custom-call(bf16[1024,256]{1,0:T(8,128)(2,1)} %bitcast.56, bf16[1024,256]{1,0:T(8,128)(2,1)} %copy-done.7, bf16[512,256]{1,0:T(8,128)(2,1)} %get-tuple-element.44.refs_2_, bf16[512,256]{1,0:T(8,128)(2,1)} %get-tuple-element.39.refs_3_), custom_call_target="tpu_custom_call" | custom-call | flops 268435456 | bytes 1048576 | tf_op jit(solution)/shard_map/pallas_call | solution.py:116
  55.5 3.3 %shard_map.278.agg_own = bf16[1024,256]{1,0:T(8,128)(2,1)} custom-call(s32[16]{0:T(128)} %send_ids.4, s32[16]{0:T(128)} %recv_ids.4, s32[1]{0:T(128)S(6)} %copy.35.live, f32[8]{0:T(128)} %get-tuple-element.51.gains, s32[16,2,128]{2,1,0:T(2,128)} %offsets.4, s32[16,128]{1,0:T(8,128)} %labels.4, f32[256,1]{1,0:T(8,128)} %copy.31.bias, ...), custom_call_target="tpu_custom_call" | custom-call | flops 268435456 | bytes 1048576 | tf_op jit(solution)/shard_map/pallas_call | solution.py:77
  59.4 1.6 collective-permute-done.4
  61.6 1.0 slice_bitcast_fusion
  63.4 8.0 %shard_map.279 = (bf16[1024,256]{1,0:T(8,128)(2,1)}, bf16[1024,256]{1,0:T(8,128)(2,1)}, bf16[8,256,128]{2,1,0:T(8,128)(2,1)}, bf16[8,256,128]{2,1,0:T(8,128)(2,1)}) custom-call(bf16[1024,256]{1,0:T(8,128)(2,1)} %shard_map.278.agg_own, bf16[1024,256]{1,0:T(8,128)(2,1)} %copy-done.8, bf16[512,256]{1,0:T(8,128)(2,1)} %get-tuple-element.43.w_own, ...), custom_call_target="tpu_custom_call" | custom-call | flops 268435456 | bytes 1048576 | tf_op jit(solution)/shard_map/pallas_call | solution.py:167
  71.5 3.2 %collective-permute-start.5 = (bf16[8,256,128]{2,1,0:T(8,128)(2,1)}, bf16[8,256,128]{2,1,0:T(8,128)(2,1)S(1)}, u32[]{:S(2)}, u32[]{:S(2)}) collective-permute-start(bf16[8,256,128]{2,1,0:T(8,128)(2,1)} %get-tuple-element.15), channel_id=1, source_target_pairs={{0,2},{2,4},{4,6},{6,8},{8,10},{10,12},{12,14},{14,16},{16,18},{18... | collective-permute-start | bytes 1572872 | tf_op jit(solution)/shard_map/ppermute | solution.py:240
  74.6 1.0 collective-permute-start.6
  77.1 10.9 %collective-permute-done.5 = bf16[8,256,128]{2,1,0:T(8,128)(2,1)S(1)} collective-permute-done((bf16[8,256,128]{2,1,0:T(8,128)(2,1)}, bf16[8,256,128]{2,1,0:T(8,128)(2,1)S(1)}, u32[]{:S(2)}, u32[]{:S(2)}) %collective-permute-start.5) | collective-permute-done | bytes 524320 | tf_op jit(solution)/shard_map/ppermute | solution.py:240
  88.8 2.4 %pad_maximum_fusion.sender = bf16[24,256,128]{2,1,0:T(8,128)(2,1)} fusion(bf16[8,256,128]{2,1,0:T(8,128)(2,1)S(1)} %collective-permute-done.6, bf16[8,256,128]{2,1,0:T(8,128)(2,1)} %get-tuple-element.15, bf16[8,256,128]{2,1,0:T(8,128)(2,1)S(1)} %collective-permute-done.5), kind=kLoop, calls=%fused_computation | loop fusion | flops 1572864 | bytes 3145728 | tf_op jit(solution)/shard_map/concatenate | solution.py:242
  91.1 7.3 %shard_map.280.agg_own = bf16[1024,256]{1,0:T(8,128)(2,1)} custom-call(s32[96]{0:T(128)} %send_ids.6, s32[96]{0:T(128)} %recv_ids.6, s32[1]{0:T(128)S(6)} %copy.36.live, f32[8]{0:T(128)} %get-tuple-element.53.gains, s32[96,2,128]{2,1,0:T(2,128)} %offsets.6, s32[96,128]{1,0:T(8,128)} %labels.6, f32[256,1]{1,0:T(8,128)} %copy.32.bias, ...), custom_call_target="tpu_custom_call" | custom-call | flops 268435456 | bytes 1048576 | tf_op jit(solution)/shard_map/pallas_call | solution.py:77
  99.0 1.5 collective-permute-done.7.agg_peer
  101.4 8.1 %shard_map.281 = (bf16[1024,256]{1,0:T(8,128)(2,1)}, bf16[1024,256]{1,0:T(8,128)(2,1)}, bf16[8,256,128]{2,1,0:T(8,128)(2,1)}, bf16[8,256,128]{2,1,0:T(8,128)(2,1)}) custom-call(bf16[1024,256]{1,0:T(8,128)(2,1)} %shard_map.280.agg_own, bf16[1024,256]{1,0:T(8,128)(2,1)} %copy-done.9, bf16[512,256]{1,0:T(8,128)(2,1)} %get-tuple-element.27.w_own, ...), custom_call_target="tpu_custom_call" | custom-call | flops 268435456 | bytes 1048576 | tf_op jit(solution)/shard_map/pallas_call | solution.py:167
  109.5 2.1 collective-permute-start.8
  111.6 2.0 collective-permute-start.9
  114.4 11.4 %collective-permute-done.8 = bf16[8,256,128]{2,1,0:T(8,128)(2,1)S(1)} collective-permute-done((bf16[8,256,128]{2,1,0:T(8,128)(2,1)}, bf16[8,256,128]{2,1,0:T(8,128)(2,1)S(1)}, u32[]{:S(2)}, u32[]{:S(2)}) %collective-permute-start.8) | collective-permute-done | bytes 524320 | tf_op jit(solution)/shard_map/ppermute | solution.py:240
  125.7 9.9 %collective-permute-done.9 = bf16[8,256,128]{2,1,0:T(8,128)(2,1)S(1)} collective-permute-done((bf16[8,256,128]{2,1,0:T(8,128)(2,1)}, bf16[8,256,128]{2,1,0:T(8,128)(2,1)S(1)}, u32[]{:S(2)}, u32[]{:S(2)}) %collective-permute-start.9) | collective-permute-done | bytes 524320 | tf_op jit(solution)/shard_map/ppermute | solution.py:241
  135.7 2.4 %pad_maximum_fusion.1.sender = bf16[24,256,128]{2,1,0:T(8,128)(2,1)} fusion(bf16[8,256,128]{2,1,0:T(8,128)(2,1)S(1)} %collective-permute-done.9, bf16[8,256,128]{2,1,0:T(8,128)(2,1)} %get-tuple-element.19, bf16[8,256,128]{2,1,0:T(8,128)(2,1)S(1)} %collective-permute-done.8), kind=kLoop, calls=%fused_computation.1 | loop fusion | flops 1572864 | bytes 3145728 | tf_op jit(solution)/shard_map/concatenate | solution.py:242
  138.1 7.3 %shard_map.282.agg_own = bf16[1024,256]{1,0:T(8,128)(2,1)} custom-call(s32[96]{0:T(128)} %send_ids.6, s32[96]{0:T(128)} %recv_ids.6, s32[1]{0:T(128)S(6)} %copy.36.live, f32[8]{0:T(128)} %get-tuple-element.53.gains, s32[96,2,128]{2,1,0:T(2,128)} %offsets.6, s32[96,128]{1,0:T(8,128)} %labels.6, f32[256,1]{1,0:T(8,128)} %copy.33.bias, ...), custom_call_target="tpu_custom_call" | custom-call | flops 268435456 | bytes 1048576 | tf_op jit(solution)/shard_map/pallas_call | solution.py:77
  148.3 7.2 %shard_map.283 = (bf16[1024,256]{1,0:T(8,128)(2,1)}, bf16[1024,256]{1,0:T(8,128)(2,1)}, bf16[8,256,128]{2,1,0:T(8,128)(2,1)}) custom-call(bf16[1024,256]{1,0:T(8,128)(2,1)} %shard_map.282.agg_own, bf16[1024,256]{1,0:T(8,128)(2,1)} %copy-done.6, bf16[512,256]{1,0:T(8,128)(2,1)} %get-tuple-element.26.w_own, bf16[512,256]{1,0:T(8,128)(2,1)} %get-tuple-element.35.w_peer, ...), custom_call_target="tpu_custom_call" | custom-call | flops 268435456 | bytes 1048576 | tf_op jit(solution)/shard_map/pallas_call | solution.py:167
  155.5 7.9 %shard_map.284.agg_own = bf16[1024,256]{1,0:T(8,128)(2,1)} custom-call(s32[24]{0:T(128)} %send_ids.7, s32[24]{0:T(128)} %recv_ids.7, s32[1]{0:T(128)S(6)} %copy.37.live, f32[8]{0:T(128)} %get-tuple-element.52.gains, s32[24,2,128]{2,1,0:T(2,128)} %offsets.7, s32[24,128]{1,0:T(8,128)} %labels.7, f32[256,1]{1,0:T(8,128)} %copy.34.bias, ...), custom_call_target="tpu_custom_call" | custom-call | flops 268435456 | bytes 1048576 | tf_op jit(solution)/shard_map/pallas_call | solution.py:77
  163.5 2.0 collective-permute-done.11.agg_peer
  166.3 5.0 %shard_map.285 = bf16[1024,256]{1,0:T(8,128)(2,1)} custom-call(bf16[1024,256]{1,0:T(8,128)(2,1)} %shard_map.284.agg_own, bf16[1024,256]{1,0:T(8,128)(2,1)} %copy-done.10, bf16[512,256]{1,0:T(8,128)(2,1)} %get-tuple-element.38.w_own, bf16[512,256]{1,0:T(8,128)(2,1)} %get-tuple-element.34.w_peer, f32[1,256]{1,0:T(1,128)} %bitcast.63), custom_call_target="tpu_custom_call" | custom-call | flops 268435456 | bytes 1048576 | tf_op jit(solution)/shard_map/pallas_call | solution.py:192
  171.4 56.8 %all_to_all.22 = bf16[128,8,256]{2,1,0:T(8,128)(2,1)} all-to-all(bf16[128,8,256]{2,1,0:T(8,128)(2,1)} %bitcast.59), channel_id=1, replica_groups=mesh['nodes'=128,'feat'=2] {'nodes'}, dimensions={0} | all-to-all | bytes 1048576 | tf_op jit(solution)/shard_map/all_to_all | solution.py:307
  228.2 3.9 %shard_map.286 = bf16[1024,256]{1,0:T(8,128)(2,1)} custom-call(s32[1,1024]{1,0:T(1,128)} %order.1, bf16[1024,256]{1,0:T(8,128)(2,1)} %bitcast.58, bf16[1024,256]{1,0:T(8,128)(2,1)} %grid.3), custom_call_target="tpu_custom_call" | custom-call | flops 268435456 | bytes 1048576 | tf_op jit(solution)/shard_map/pallas_call | solution.py:229
  (60 shorter events, 13.4 us)
Async XLA Ops:
  0.6 21.6 %copy-start.4 = (bf16[3,512,256]{2,1,0:T(8,128)(2,1)S(1)}, bf16[3,512,256]{2,1,0:T(8,128)(2,1)}, u32[]{:S(2)}) copy-start(bf16[3,512,256]{2,1,0:T(8,128)(2,1)} %param.47) | copy-start | bytes 2359300
  6.6 16.5 %copy-start.5 = (bf16[3,512,256]{2,1,0:T(8,128)(2,1)S(1)}, bf16[3,512,256]{2,1,0:T(8,128)(2,1)}, u32[]{:S(2)}) copy-start(bf16[3,512,256]{2,1,0:T(8,128)(2,1)} %param.49) | copy-start | bytes 2359300
  6.6 35.7 %all-to-all-start = ((bf16[128,8,256]{2,1,0:T(8,128)(2,1)}), bf16[128,8,256]{2,1,0:T(8,128)(2,1)S(1)}, u32[]{:S(2)}, u32[]{:S(2)}) async-start(bf16[128,8,256]{2,1,0:T(8,128)(2,1)} %bitcast.57), calls=%async_computation | async-start | bytes 1048576 | tf_op jit(solution)/shard_map/all_to_all | solution.py:276
  22.2 1.8 copy-start.3
  25.2 1.1 copy-start.1
  25.2 17.2 %copy-start.16 = (f32[256]{0:T(256)S(1)}, f32[256]{0:T(256)}, u32[]{:S(2)}) copy-start(f32[256]{0:T(256)} %param.50) | copy-start | bytes 3076
  25.2 18.7 %copy-start.15 = (f32[3,8]{1,0:T(4,128)S(1)}, f32[3,8]{1,0:T(4,128)}, u32[]{:S(2)}) copy-start(f32[3,8]{1,0:T(4,128)} %param.46) | copy-start | bytes 292
  26.3 35.3 %collective-permute-start.3 = (bf16[4,512,256]{2,1,0:T(8,128)(2,1)}, bf16[4,512,256]{2,1,0:T(8,128)(2,1)S(1)}, u32[]{:S(2)}, u32[]{:S(2)}) collective-permute-start(bf16[4,512,256]{2,1,0:T(8,128)(2,1)} %pad_maximum_fusion.2), channel_id=1, source_target_pairs={{0,1},{1,0},{2,3},{3,2},{4,5},{5,4},{6,7},{7,6},{8,9},{9,8},{10,11... | collective-permute-start | bytes 3145736 | tf_op jit(solution)/shard_map/ppermute | solution.py:233
  26.3 18.1 %collective-permute-start.1 = (bf16[1024,256]{1,0:T(8,128)(2,1)S(1)}, bf16[1024,256]{1,0:T(8,128)(2,1)S(1)}, u32[]{:S(2)}, u32[]{:S(2)}) collective-permute-start(bf16[1024,256]{1,0:T(8,128)(2,1)S(1)} %copy-done.1), channel_id=1, source_target_pairs={{0,1},{1,0},{2,3},{3,2},{4,5},{5,4},{6,7},{7,6},{8,9},{9,8},{10,11... | collective-permute-start | bytes 1572872 | tf_op jit(solution)/shard_map/ppermute | solution.py:233
  42.4 7.1 %copy-start = (bf16[128,8,256]{2,1,0:T(8,128)(2,1)}, bf16[128,8,256]{2,1,0:T(8,128)(2,1)S(1)}, u32[]{:S(2)}) copy-start(bf16[128,8,256]{2,1,0:T(8,128)(2,1)S(1)} %all-to-all-done) | copy-start | bytes 1572868
  42.4 7.1 %collective-permute-start = (bf16[1024,256]{1,0:T(8,128)(2,1)S(1)}, bf16[1024,256]{1,0:T(8,128)(2,1)S(1)}, u32[]{:S(2)}, u32[]{:S(2)}) collective-permute-start(bf16[1024,256]{1,0:T(8,128)(2,1)S(1)} %bitcast.55), channel_id=1, source_target_pairs={{0,1},{1,0},{2,3},{3,2},{4,5},{5,4},{6,7},{7,6},{8,9},{9,8},{10,11... | collective-permute-start | bytes 1572872 | tf_op jit(solution)/shard_map/ppermute | solution.py:233
  44.5 0.8 copy-start.2
  49.5 0.8 copy-start.7
  50.3 8.9 %copy-start.11 = (f32[2,256]{1,0:T(2,128)S(1)}, f32[2,256]{1,0:T(2,128)}, u32[]{:S(2)}) copy-start(f32[2,256]{1,0:T(2,128)} %param.53) | copy-start | bytes 6148
  50.3 8.9 %copy-start.12 = (f32[256]{0:T(256)S(1)}, f32[256]{0:T(256)}, u32[]{:S(2)}) copy-start(f32[256]{0:T(256)} %param.51) | copy-start | bytes 3076
  50.3 8.9 %copy-start.13 = (f32[256]{0:T(256)S(1)}, f32[256]{0:T(256)}, u32[]{:S(2)}) copy-start(f32[256]{0:T(256)} %param.55) | copy-start | bytes 3076
  58.8 3.8 %collective-permute-start.2 = (bf16[1024,256]{1,0:T(8,128)(2,1)}, bf16[1024,256]{1,0:T(8,128)(2,1)S(1)}, u32[]{:S(2)}, u32[]{:S(2)}) collective-permute-start(bf16[1024,256]{1,0:T(8,128)(2,1)} %shard_map.278.agg_own), channel_id=1, source_target_pairs={{0,1},{1,0},{2,3},{3,2},{4,5},{5,4},{6,7},{7,6},{8,9},{9,8},{10,11... | collective-permute-start | bytes 1572872 | tf_op jit(solution)/shard_map/ppermute | solution.py:233
  59.3 1.7 collective-permute-start.4
  62.6 0.8 copy-start.8
  63.4 12.2 %copy-start.14 = (f32[2,256]{1,0:T(2,128)S(1)}, f32[2,256]{1,0:T(2,128)}, u32[]{:S(2)}) copy-start(f32[2,256]{1,0:T(2,128)} %param.52) | copy-start | bytes 6148
  71.5 16.5 %collective-permute-start.5 = (bf16[8,256,128]{2,1,0:T(8,128)(2,1)}, bf16[8,256,128]{2,1,0:T(8,128)(2,1)S(1)}, u32[]{:S(2)}, u32[]{:S(2)}) collective-permute-start(bf16[8,256,128]{2,1,0:T(8,128)(2,1)} %get-tuple-element.15), channel_id=1, source_target_pairs={{0,2},{2,4},{4,6},{6,8},{8,10},{10,12},{12,14},{14,16},{16,18},{18... | collective-permute-start | bytes 1572872 | tf_op jit(solution)/shard_map/ppermute | solution.py:240
  74.6 14.1 %collective-permute-start.6 = (bf16[8,256,128]{2,1,0:T(8,128)(2,1)}, bf16[8,256,128]{2,1,0:T(8,128)(2,1)S(1)}, u32[]{:S(2)}, u32[]{:S(2)}) collective-permute-start(bf16[8,256,128]{2,1,0:T(8,128)(2,1)} %get-tuple-element.15), channel_id=1, source_target_pairs={{2,0},{4,2},{6,4},{8,6},{10,8},{12,10},{14,12},{16,14},{18,16},{20... | collective-permute-start | bytes 1572872 | tf_op jit(solution)/shard_map/ppermute | solution.py:241
  98.5 2.1 collective-permute-start.7
  100.6 0.8 copy-start.9
  109.5 16.3 %collective-permute-start.8 = (bf16[8,256,128]{2,1,0:T(8,128)(2,1)}, bf16[8,256,128]{2,1,0:T(8,128)(2,1)S(1)}, u32[]{:S(2)}, u32[]{:S(2)}) collective-permute-start(bf16[8,256,128]{2,1,0:T(8,128)(2,1)} %get-tuple-element.19), channel_id=1, source_target_pairs={{0,2},{2,4},{4,6},{6,8},{8,10},{10,12},{12,14},{14,16},{16,18},{18... | collective-permute-start | bytes 1572872 | tf_op jit(solution)/shard_map/ppermute | solution.py:240
  111.6 24.1 %collective-permute-start.9 = (bf16[8,256,128]{2,1,0:T(8,128)(2,1)}, bf16[8,256,128]{2,1,0:T(8,128)(2,1)S(1)}, u32[]{:S(2)}, u32[]{:S(2)}) collective-permute-start(bf16[8,256,128]{2,1,0:T(8,128)(2,1)} %get-tuple-element.19), channel_id=1, source_target_pairs={{2,0},{4,2},{6,4},{8,6},{10,8},{12,10},{14,12},{16,14},{18,16},{20... | collective-permute-start | bytes 1572872 | tf_op jit(solution)/shard_map/ppermute | solution.py:241
  138.1 7.3 %copy-start.17 = (f32[256]{0:T(256)S(1)}, f32[256]{0:T(256)}, u32[]{:S(2)}) copy-start(f32[256]{0:T(256)} %param.54) | copy-start | bytes 3076
  145.4 2.1 collective-permute-start.10
  147.5 0.8 copy-start.6
  163.4 2.1 collective-permute-start.11
  165.5 0.8 copy-start.10

commit v2 on v1

v2 whole, which is shorter than its diff:
```python
import functools

import jax
import jax.numpy as jnp
from jax import lax
from jax.experimental import pallas as pl
from jax.experimental.pallas import tpu as pltpu
from jax.sharding import PartitionSpec as P

D = 512
BLOCK = 128
ROUNDS = 2
NCLASS = 8
EPS = 1e-05
F32 = jnp.float32
BF16 = jnp.bfloat16

VMEM = pl.BlockSpec(memory_space=pltpu.VMEM)
SMEM = pl.BlockSpec(memory_space=pltpu.SMEM)


def call(kernel, ins, outs, scratch=(), flops=1 << 28, **params):
    return pl.pallas_call(
        kernel,
        in_specs=ins,
        out_specs=[VMEM] * len(outs) if isinstance(outs, (list, tuple)) else VMEM,
        out_shape=outs,
        scratch_shapes=list(scratch),
        cost_estimate=pl.CostEstimate(flops=flops, bytes_accessed=1 << 20, transcendentals=0),
        compiler_params=pltpu.CompilerParams(**params),
    )


def dot(a, b, dims=((1,), (0,))):
    return lax.dot_general(a, b, (dims, ((), ())), preferred_element_type=F32)


def edge_kernel(unroll, gain_row, bias_row, send_ids, recv_ids, live, gains, offsets, labels, bias, sender, receiver, out, total, high, low):
    slots = labels.shape[0]
    blocks = total.shape[0]
    chosen = labels[...]
    weight = jnp.zeros((slots, BLOCK), F32)
    for c in range(NCLASS):
        weight = jnp.where(chosen == c, gains[gain_row, c], weight)
    alive = lax.broadcasted_iota(jnp.int32, (slots, BLOCK), 0) < live[0]
    weight = jnp.where(alive, weight, 0.0)
    top = weight.astype(BF16).astype(F32)
    high[...] = top
    low[...] = weight - top
    total[...] = jnp.zeros_like(total)
    shift = bias[bias_row : bias_row + 1, :] * 0.5
    rows = lax.broadcasted_iota(jnp.int32, (BLOCK, BLOCK), 0)

    def turn(t, carry):
        sums = []
        for u in range(unroll):
            k = t * unroll + u
            pair = offsets[k]
            from_is = rows == pair[0:1, :]
            to_is = rows == pair[1:2, :]
            hot = jnp.concatenate([jnp.where(from_is, 0.5, 0.0), jnp.where(to_is, 0.5, 0.0)], axis=0).astype(BF16)
            both = jnp.concatenate([sender[send_ids[k]], receiver[recv_ids[k]]], axis=0)
            half = dot(hot, both, ((0,), (0,))) + shift
            message = (half * (1.0 + jnp.tanh(half))).astype(BF16)
            back = jnp.concatenate(
                [jnp.where(to_is, high[pl.ds(k, 1), :], 0.0), jnp.where(to_is, low[pl.ds(k, 1), :], 0.0)], axis=1
            ).astype(BF16)
            sums.append(dot(back, jnp.concatenate([message, message], axis=0)))
        for u in range(unroll):
            taker = recv_ids[t * unroll + u]
            total[taker] = total[taker] + sums[u]
        return carry

    lax.fori_loop(0, (live[0] + unroll - 1) // unroll, turn, 0)
    for b in range(blocks):
        out[b * BLOCK : (b + 1) * BLOCK, :] = total[b].astype(BF16)


def edge_sum(sender, receiver, bias, bias_row, gains, gain_row, send_ids, recv_ids, offsets, labels, live, unroll):
    slots = labels.shape[0]
    blocks, _, width = receiver.shape
    return call(
        functools.partial(edge_kernel, unroll, gain_row, bias_row),
        [SMEM] * 4 + [VMEM] * 5,
        jax.ShapeDtypeStruct((blocks * BLOCK, width), BF16),
        [
            pltpu.VMEM((blocks, BLOCK, width), F32),
            pltpu.VMEM((slots, BLOCK), F32),
            pltpu.VMEM((slots, BLOCK), F32),
        ],
    )(send_ids, recv_ids, live, gains, offsets, labels, bias, sender, receiver)


PIECE = 256
DMA = pltpu.SemaphoreType.DMA
MESH_ID = pl.DeviceIdType.MESH


def meet(partners):
    barrier = pltpu.get_barrier_semaphore()
    for partner in partners:
        pl.semaphore_signal(barrier, inc=1, device_id=partner, device_id_type=MESH_ID)
    pl.semaphore_wait(barrier, len(partners))


def remote(source, target, send_sem, recv_sem, partner):
    return pltpu.make_async_remote_copy(
        src_ref=source, dst_ref=target, send_sem=send_sem, recv_sem=recv_sem,
        device_id=partner, device_id_type=MESH_ID,
    )


def rows_of(c):
    return pl.ds(pl.multiple_of(c * PIECE, PIECE), PIECE)


def ordered(matrix, feat):
    half = matrix.shape[0] // 2
    own = matrix[pl.ds(pl.multiple_of(feat * half, half), half), :]
    peer = matrix[pl.ds(pl.multiple_of((1 - feat) * half, half), half), :]
    return jnp.concatenate([own, peer], axis=0)


def put(out, c, value):
    per = PIECE // BLOCK
    for i in range(per):
        out[c * per + i] = value[i * BLOCK : (i + 1) * BLOCK, :].astype(BF16)


def normed(mixed_own, mixed_peer, gain_own, gain_peer):
    total = jnp.sum(mixed_own, axis=1, keepdims=True) + jnp.sum(mixed_peer, axis=1, keepdims=True)
    square = jnp.sum(mixed_own * mixed_own, axis=1, keepdims=True) + jnp.sum(
        mixed_peer * mixed_peer, axis=1, keepdims=True
    )
    average = total * (1.0 / D)
    spread = square * (1.0 / D) - average * average
    scale = lax.rsqrt(spread + EPS)
    mine = (mixed_own - average) * scale * gain_own
    if gain_peer is None:
        return mine, None
    return mine, (mixed_peer - average) * scale * gain_peer


def setup_kernel(enc, first, second, dec, enc_gain, mesh_gain, own, outer, enc_gain_peer, mesh_gain_peer, peer, take, *sems):
    feat = lax.axis_index("feat")
    partner = {"feat": 1 - feat}
    meet([partner])
    send_sems, recv_sems = sems
    pieces = own.shape[0] // PIECE
    moves = [(own.at[pl.ds(c * PIECE, PIECE)], peer.at[pl.ds(c * PIECE, PIECE)]) for c in range(pieces)]
    moves += [(enc.at[2], outer.at[0]), (first.at[0, 2], outer.at[1]), (second.at[0, 2], outer.at[2]), (dec.at[2], outer.at[3])]
    moves += [(enc_gain, enc_gain_peer), (mesh_gain, mesh_gain_peer)]
    copies = [remote(s, t, send_sems.at[i], recv_sems.at[i], partner) for i, (s, t) in enumerate(moves)]
    for copy in copies:
        copy.start()
    weight = ordered(enc.at[1], feat)
    for c in range(pieces):
        copies[c].wait_recv()
        rows = rows_of(c)
        put(take, c, dot(jnp.concatenate([own[rows, :], peer[rows, :]], axis=1), weight))
    for copy in copies[pieces:]:
        copy.wait_recv()
    for copy in copies:
        copy.wait_send()


def setup(enc, mesh_w, dec, enc_gain, mesh_gain, own):
    rows, width = own.shape
    count = rows // PIECE + 6
    shape = jax.ShapeDtypeStruct
    return call(
        setup_kernel,
        [VMEM] * 7,
        [
            shape((4, D, width), BF16),
            shape((1, width), F32),
            shape((ROUNDS, width), F32),
            shape((rows, width), BF16),
            shape((rows // BLOCK, BLOCK, width), BF16),
        ],
        [DMA((count,)), DMA((count,))],
        collective_id=0,
        has_side_effects=True,
    )(enc, mesh_w[0:1], mesh_w[1:2], dec, enc_gain, mesh_gain, own)


def exchange(own, peer, send_sems, recv_sems, partner):
    return [
        remote(own.at[pl.ds(c * PIECE, PIECE)], peer.at[pl.ds(c * PIECE, PIECE)], send_sems.at[c], recv_sems.at[c], partner)
        for c in range(own.shape[0] // PIECE)
    ]


def grid_kernel(own, enc, dec, sides, takes, peer, send_sems, recv_sems):
    feat = lax.axis_index("feat")
    partner = {"feat": 1 - feat}
    meet([partner])
    copies = exchange(own, peer, send_sems, recv_sems, partner)
    for copy in copies:
        copy.start()
    first, second = ordered(enc.at[0], feat), ordered(dec.at[1], feat)
    for c, copy in enumerate(copies):
        copy.wait_recv()
        rows = rows_of(c)
        both = jnp.concatenate([own[rows, :], peer[rows, :]], axis=1)
        put(sides, c, dot(both, first))
        put(takes, c, dot(both, second))
    for copy in copies:
        copy.wait_send()


def grid_sides(own, enc, dec):
    rows, width = own.shape
    shape = jax.ShapeDtypeStruct((rows // BLOCK, BLOCK, width), BF16)
    count = rows // PIECE
    return call(
        grid_kernel,
        [VMEM] * 3,
        [shape, shape],
        [pltpu.VMEM((rows, width), BF16), DMA((count,)), DMA((count,))],
        collective_id=1,
        has_side_effects=True,
    )(own, enc, dec)


def refresh_kernel(near, stage, gain_row, agg, w_own, w_peer, gain_own, gain_peer, mesh_own, mesh_peer, following, new_own, new_peer, sent, *refs):
    feat = lax.axis_index("feat")
    partner = {"feat": 1 - feat}
    if near:
        take, peer, send_sems, recv_sems, up_send, up_recv, down_send, down_recv = refs
        node, size = lax.axis_index("nodes"), lax.axis_size("nodes")
        after = {"nodes": lax.rem(node + 1, size)}
        before = {"nodes": lax.rem(node + size - 1, size)}
        meet([partner, before, after])
    else:
        peer, send_sems, recv_sems = refs
        meet([partner])
    copies = exchange(agg, peer, send_sems, recv_sems, partner)
    for copy in copies:
        copy.start()
    pieces = len(copies)
    per = PIECE // BLOCK
    blocks = pieces * per
    shift = blocks if near else 0
    outgoing = []
    if near:
        for c in range(pieces):
            here = sent.at[pl.ds(blocks + c * per, per)]
            outgoing.append(remote(here, sent.at[pl.ds(c * per, per)], up_send.at[c], up_recv.at[c], after))
            outgoing.append(remote(here, sent.at[pl.ds(2 * blocks + c * per, per)], down_send.at[c], down_recv.at[c], before))
    mine, theirs = ordered(w_own, feat), ordered(w_peer, feat)
    for c, copy in enumerate(copies):
        copy.wait_recv()
        rows = rows_of(c)
        both = jnp.concatenate([agg[rows, :], peer[rows, :]], axis=1)
        own, other = normed(
            dot(both, mine), dot(both, theirs), gain_own[gain_row : gain_row + 1, :], gain_peer[gain_row : gain_row + 1, :]
        )
        own = (mesh_own[rows, :].astype(F32) + own).astype(BF16)
        other = (mesh_peer[rows, :].astype(F32) + other).astype(BF16)
        new_own[rows, :] = own
        new_peer[rows, :] = other
        both = jnp.concatenate([own, other], axis=1)
        put(sent.at[pl.ds(shift, blocks)], c, dot(both, ordered(following.at[0], feat)))
        if near:
            if c:
                outgoing[2 * c - 2].start()
                outgoing[2 * c - 1].start()
            put(take, c, dot(both, ordered(following.at[1], feat)))
    for copy in outgoing[2 * pieces - 2 :]:
        copy.start()
    for copy in outgoing:
        copy.wait_recv()
    for copy in copies + outgoing:
        copy.wait_send()


def refresh(stage, near, agg, w_own, w_peer, gain_own, gain_peer, gain_row, mesh_own, mesh_peer, following):
    rows, width = agg.shape
    blocks, count = rows // BLOCK, rows // PIECE
    shape = jax.ShapeDtypeStruct
    outs = [shape((rows, width), BF16)] * 2 + [shape((blocks * (3 if near else 1), BLOCK, width), BF16)]
    scratch = [pltpu.VMEM((rows, width), BF16), DMA((count,)), DMA((count,))]
    if near:
        outs.append(shape((blocks, BLOCK, width), BF16))
        scratch += [DMA((count,))] * 4
    return call(
        functools.partial(refresh_kernel, near, stage, gain_row),
        [VMEM] * 8,
        outs,
        scratch,
        collective_id=2 + stage,
        has_side_effects=True,
    )(agg, w_own, w_peer, gain_own, gain_peer, mesh_own, mesh_peer, following)


def update_kernel(agg, w_own, w_peer, gain_own, out, peer, send_sems, recv_sems):
    feat = lax.axis_index("feat")
    partner = {"feat": 1 - feat}
    meet([partner])
    copies = exchange(agg, peer, send_sems, recv_sems, partner)
    for copy in copies:
        copy.start()
    mine, theirs = ordered(w_own, feat), ordered(w_peer, feat)
    for c, copy in enumerate(copies):
        copy.wait_recv()
        rows = rows_of(c)
        both = jnp.concatenate([agg[rows, :], peer[rows, :]], axis=1)
        own, _ = normed(dot(both, mine), dot(both, theirs), gain_own[...], None)
        out[rows, :] = own.astype(BF16)
    for copy in copies:
        copy.wait_send()


def update_of(agg, w_own, w_peer, gain_own):
    rows, width = agg.shape
    count = rows // PIECE
    return call(
        update_kernel,
        [VMEM] * 4,
        jax.ShapeDtypeStruct(agg.shape, BF16),
        [pltpu.VMEM((rows, width), BF16), DMA((count,)), DMA((count,))],
        collective_id=6,
        has_side_effects=True,
    )(agg, w_own, w_peer, gain_own)


def pick_kernel(order, grid, out):
    rows = grid.shape[0]
    spot = lax.broadcasted_iota(jnp.int32, (rows, BLOCK), 0)

    def step(b, carry):
        here = pl.ds(pl.multiple_of(b * BLOCK, BLOCK), BLOCK)
        hot = jnp.where(spot == order[:, here], 1.0, 0.0).astype(BF16)
        out[here, :] = dot(hot, grid[...], ((0,), (0,))).astype(BF16)
        return carry

    lax.fori_loop(0, rows // BLOCK, step, 0, unroll=2)


def pick(order, grid):
    return call(pick_kernel, [VMEM] * 2, jax.ShapeDtypeStruct(grid.shape, BF16))(order, grid)


def place_kernel(order, returned, grid, out):
    rows = grid.shape[0]

    def step(b, carry):
        start = pl.multiple_of(b * PIECE, PIECE)
        here = pl.ds(start, PIECE)
        spot = lax.broadcasted_iota(jnp.int32, (PIECE, rows), 0) + start
        hot = jnp.where(spot == order[...], 1.0, 0.0).astype(BF16)
        out[here, :] = (grid[here, :].astype(F32) + dot(hot, returned[...])).astype(BF16)
        return carry

    lax.fori_loop(0, rows // PIECE, step, 0, unroll=2)


def place(order, returned, grid):
    return call(place_kernel, [VMEM] * 3, jax.ShapeDtypeStruct(grid.shape, BF16))(order, returned, grid)


def local(
    grid_latent,
    mesh_latent,
    grid_order,
    enc_send_block,
    enc_recv_block,
    enc_offsets,
    enc_classes,
    enc_live,
    mesh_send_block,
    mesh_recv_block,
    mesh_offsets,
    mesh_classes,
    mesh_live,
    dec_send_block,
    dec_recv_block,
    dec_offsets,
    dec_classes,
    dec_live,
    class_gain,
    enc_weights,
    mesh_weights,
    dec_weights,
    enc_bias,
    enc_gain,
    mesh_bias,
    mesh_gain,
    dec_bias,
    dec_gain,
):
    arrived = lax.all_to_all(pick(grid_order, grid_latent), "nodes", split_axis=0, concat_axis=0, tiled=True)
    outer_peer, enc_gain_peer, mesh_gain_peer, mesh_peer, mesh_take = setup(
        enc_weights, mesh_weights, dec_weights, enc_gain[None, :], mesh_gain, mesh_latent
    )
    mesh_own = mesh_latent
    grid_send, grid_take = grid_sides(arrived, enc_weights, dec_weights)
    agg = edge_sum(
        grid_send, mesh_take, enc_bias[None, :], 0, class_gain, 0,
        enc_send_block, enc_recv_block, enc_offsets, enc_classes, enc_live, 8,
    )
    mesh_own, mesh_peer, nearby, taking = refresh(
        0, True, agg, enc_weights[2], outer_peer[0], enc_gain[None, :], enc_gain_peer, 0,
        mesh_own, mesh_peer, mesh_weights[0, 0:2],
    )
    for index in range(ROUNDS):
        agg = edge_sum(
            nearby, taking, mesh_bias, index, class_gain, 1,
            mesh_send_block, mesh_recv_block, mesh_offsets, mesh_classes, mesh_live, 16,
        )
        last = index == ROUNDS - 1
        following = dec_weights[0:1] if last else mesh_weights[index + 1, 0:2]
        mesh_own, mesh_peer, *sides = refresh(
            index + 1, not last, agg, mesh_weights[index, 2], outer_peer[index + 1], mesh_gain, mesh_gain_peer, index,
            mesh_own, mesh_peer, following,
        )
        if not last:
            nearby, taking = sides
    (dec_send,) = sides
    agg = edge_sum(
        dec_send, grid_take, dec_bias[None, :], 0, class_gain, 2,
        dec_send_block, dec_recv_block, dec_offsets, dec_classes, dec_live, 12,
    )
    update = update_of(agg, dec_weights[2], outer_peer[3], dec_gain[None, :])
    returned = lax.all_to_all(update, "nodes", split_axis=0, concat_axis=0, tiled=True)
    return (place(grid_order, returned, grid_latent), mesh_own)


def solution(mesh):
    in_specs = (
        P("nodes", "feat"),
        P("nodes", "feat"),
        P("nodes", None),
        P("nodes"),
        P("nodes"),
        P("nodes", None, None),
        P("nodes", None),
        P("nodes"),
        P("nodes"),
        P("nodes"),
        P("nodes", None, None),
        P("nodes", None),
        P("nodes"),
        P("nodes"),
        P("nodes"),
        P("nodes", None, None),
        P("nodes", None),
        P("nodes"),
        P(),
        P(None, None, "feat"),
        P(None, None, None, "feat"),
        P(None, None, "feat"),
        P("feat"),
        P("feat"),
        P(None, "feat"),
        P(None, "feat"),
        P("feat"),
        P("feat"),
    )
    out_specs = (P("nodes", "feat"), P("nodes", "feat"))
    return jax.shard_map(local, mesh=mesh, in_specs=in_specs, out_specs=out_specs, check_vma=False)
```

time: 236 us -> 165 us (0.70)
  blocking collectives: 56.8 us -> 0 us
  waiting for transfers between devices: 54.3 us -> 25.4 us
  Pallas kernels: 71.7 us -> 92.1 us
  starting transfers between devices: 25.1 us -> 34.4 us
  local copies, waits for them, and re-layouts: 15.6 us -> 8.49 us
  other arithmetic: 5.9 us -> 0 us
    all_to_all x1 -> x0, blocking collectives: 56.8 us -> none  [local(): lax.all_to_all(update, 'nodes', split_axis=0, concat_axis=0, tiled=True)]
    ppermute x12 -> x0, waiting for transfers between devices: 38.8 us -> none  [the longest x2 22.3 us: neighbours(): before = lax.ppermute(value, 'nodes', up)]
    pallas_call x10, Pallas kernels: 63.6 us -> 85.8 us  [the longest x3 54.4 us: refresh(): call(functools.partial(refresh_kernel, near, stage, gain_row), [VMEM] * 8...]
    all_to_all x1 -> x2, starting transfers between devices: 15.6 us -> 34.4 us  [the longest x1 19 us: local(): lax.all_to_all(update, 'nodes', split_axis=0, concat_axis=0, tiled=True)]
    all_to_all x1 -> x2, waiting for transfers between devices: 15.5 us -> 25.4 us  [the longest x1 20.5 us: local(): lax.all_to_all(update, 'nodes', split_axis=0, concat_axis=0, tiled=True)]
    ppermute x12 -> x0, starting transfers between devices: 9.52 us -> none  [the longest x2 5.32 us: neighbours(): before = lax.ppermute(value, 'nodes', up)]
    another operation x6 -> x0, local copies, waits for them, and re-layouts: 5.45 us -> none  [the longest x1 1.78 us: pick(): order[:, None]]
    concatenate x2 -> x0, other arithmetic: 4.77 us -> none  [neighbours(): return jnp.concatenate([before, value, after], axis=0)]
  transfers between devices with their start and end apart: 13 -> 2, of which waited for: 9 -> 2; matrix products, arithmetic and copies ran while one was open for 4% -> 4% of each run, Pallas kernels for 5% -> 4%
where the time goes in v2:
time: 165 us; the launch traced here: 163 us
  Pallas kernels  92.1 us (56%)
  starting transfers between devices  34.4 us (21%)
  waiting for transfers between devices  25.4 us (15%)
  local copies, waits for them, and re-layouts  8.49 us (5%)
  between operations  2.69 us (2%)
    pallas_call x3, Pallas kernels, refresh(): call(functools.partial(refresh_kernel, near, stage, gain_row), [VMEM] * 8...  54.4 us
    all_to_all x1, waiting for transfers between devices, local(): lax.all_to_all(update, 'nodes', split_axis=0, concat_axis=0, tiled=True)  20.5 us
    all_to_all x1, starting transfers between devices, local(): lax.all_to_all(update, 'nodes', split_axis=0, concat_axis=0, tiled=True)  19 us
    all_to_all x1, starting transfers between devices, local(): lax.all_to_all(pick(grid_order, grid_latent), 'nodes', split_axis=0, conc...  15.4 us
    pallas_call x4, Pallas kernels, edge_sum(): call(functools.partial(edge_kernel, unroll, gain_row, bias_row), [SMEM] *...  13.8 us
    pallas_call x1, Pallas kernels, setup(): call(setup_kernel, [VMEM] * 7, [shape((4, D, width), BF16), shape((1, wid...  7.17 us
    pallas_call x1, Pallas kernels, update_of(): call(update_kernel, [VMEM] * 4, jax.ShapeDtypeStruct(agg.shape, BF16), [p...  5.25 us
    pallas_call x1, Pallas kernels, grid_sides(): call(grid_kernel, [VMEM] * 3, [shape, shape], [pltpu.VMEM((rows, width),...  5.14 us
  transfers between devices with their start and end apart: 2, of which 2 were waited for; matrix products, arithmetic and copies ran while one was open for 4% of the time, Pallas kernels for 4%

profile of v2, /device:TPU:2, one launch (start us, length us, event | category | flops | bytes accessed | tf_op | source)
XLA Modules:
  0.0 163.0 jit_solution(4746494955308221043)
XLA Ops:
  0.6 0.0 copy-start
  0.6 3.4 %shard_map.275 = bf16[1024,256]{1,0:T(8,128)(2,1)} custom-call(s32[1,1024]{1,0:T(1,128)} %order.3, bf16[1024,256]{1,0:T(8,128)(2,1)} %grid.3), custom_call_target="tpu_custom_call" | custom-call | flops 268435456 | bytes 1048576 | tf_op jit(solution)/shard_map/pallas_call | solution.py:342
  4.0 15.4 %all-to-all-start = ((bf16[128,8,256]{2,1,0:T(8,128)(2,1)}), bf16[128,8,256]{2,1,0:T(8,128)(2,1)S(1)}, u32[]{:S(2)}, u32[]{:S(2)}) async-start(bf16[128,8,256]{2,1,0:T(8,128)(2,1)} %bitcast.29), calls=%async_computation | async-start | bytes 1048576 | tf_op jit(solution)/shard_map/all_to_all | solution.py:393
  19.4 0.0 copy-done
  19.4 1.2 fusion
  22.6 0.0 copy-start.1
  22.7 7.2 %shard_map.277 = (bf16[4,512,256]{2,1,0:T(8,128)(2,1)}, f32[1,256]{1,0:T(1,128)}, f32[2,256]{1,0:T(2,128)}, bf16[1024,256]{1,0:T(8,128)(2,1)}, bf16[8,128,256]{2,1,0:T(8,128)(2,1)}) custom-call(bf16[3,512,256]{2,1,0:T(8,128)(2,1)} %enc.3, bf16[1,3,512,256]{3,2,1,0:T(8,128)(2,1)} %get-tuple-element.41.first, ...), custom_call_target="tpu_custom_call" | custom-call | flops 268435456 | bytes 1048576 | tf_op jit(solution)/shard_map/pallas_call | solution.py:171
  29.8 0.0 copy-done.1
  29.8 0.9 slice_bitcast_fusion.3
  30.7 0.0 copy-start.4
  30.7 0.9 slice_bitcast_fusion.5
  31.6 1.0 slice_bitcast_fusion
  32.6 0.0 copy-done.4
  32.6 2.1 %slice_bitcast_fusion.2 = (bf16[512,256]{1,0:T(8,128)(2,1)}, bf16[512,256]{1,0:T(8,128)(2,1)}, bf16[512,256]{1,0:T(8,128)(2,1)}, bf16[512,256]{1,0:T(8,128)(2,1)}, bf16[512,256]{1,0:T(8,128)(2,1)}) fusion(bf16[4,512,256]{2,1,0:T(8,128)(2,1)S(1)} %copy-done.4, bf16[3,512,256]{2,1,0:T(8,128)(2,1)} %enc.3), kind=kLoop, calls=%fused_computation.2 | loop fusion | bytes 2621440 | tf_op jit(solution)/shard_map/squeeze | solution.py:425
  34.7 4.9 %all-to-all-done = bf16[128,8,256]{2,1,0:T(8,128)(2,1)S(1)} async-done(((bf16[128,8,256]{2,1,0:T(8,128)(2,1)}), bf16[128,8,256]{2,1,0:T(8,128)(2,1)S(1)}, u32[]{:S(2)}, u32[]{:S(2)}) %all-to-all-start) | async-done | bytes 524320 | tf_op jit(solution)/shard_map/all_to_all | solution.py:393
  39.6 0.8 copy-done.3
  40.4 5.1 %shard_map.276 = (bf16[8,128,256]{2,1,0:T(8,128)(2,1)}, bf16[8,128,256]{2,1,0:T(8,128)(2,1)}) custom-call(bf16[1024,256]{1,0:T(8,128)(2,1)} %bitcast.30, bf16[3,512,256]{2,1,0:T(8,128)(2,1)} %enc.3, bf16[3,512,256]{2,1,0:T(8,128)(2,1)} %dec.3), custom_call_target="tpu_custom_call" | custom-call | flops 268435456 | bytes 1048576 | tf_op jit(solution)/shard_map/pallas_call | solution.py:216
  45.5 2.8 %shard_map.278.agg = bf16[1024,256]{1,0:T(8,128)(2,1)} custom-call(s32[16]{0:T(128)} %send_ids.4, s32[16]{0:T(128)} %recv_ids.4, s32[1]{0:T(128)S(6)} %copy.31.live, f32[3,8]{1,0:T(4,128)} %gains.7, s32[16,2,128]{2,1,0:T(2,128)} %offsets.4, s32[16,128]{1,0:T(8,128)} %labels.4, f32[1,256]{1,0:T(1,128)} %bitcast.35, ...), custom_call_target="tpu_custom_call" | custom-call | flops 268435456 | bytes 1048576 | tf_op jit(solution)/shard_map/pallas_call | solution.py:82
  48.4 22.3 %shard_map.279 = (bf16[1024,256]{1,0:T(8,128)(2,1)}, bf16[1024,256]{1,0:T(8,128)(2,1)}, bf16[24,128,256]{2,1,0:T(8,128)(2,1)}, bf16[8,128,256]{2,1,0:T(8,128)(2,1)}) custom-call(bf16[1024,256]{1,0:T(8,128)(2,1)} %shard_map.278.agg, bf16[512,256]{1,0:T(8,128)(2,1)} %get-tuple-element.48.w_own, bf16[512,256]{1,0:T(8,128)(2,1)} %get-tuple-element.45.w_peer, ...), custom_call_target="tpu_custom_call" | custom-call | flops 268435456 | bytes 1048576 | tf_op jit(solution)/shard_map/pallas_call | solution.py:287
  70.7 3.5 %shard_map.280.agg = bf16[1024,256]{1,0:T(8,128)(2,1)} custom-call(s32[96]{0:T(128)} %send_ids.6, s32[96]{0:T(128)} %recv_ids.6, s32[1]{0:T(128)S(6)} %copy.32.live, f32[3,8]{1,0:T(4,128)} %gains.7, s32[96,2,128]{2,1,0:T(2,128)} %offsets.6, s32[96,128]{1,0:T(8,128)} %labels.6, f32[2,256]{1,0:T(2,128)} %bias.3, ...), custom_call_target="tpu_custom_call" | custom-call | flops 268435456 | bytes 1048576 | tf_op jit(solution)/shard_map/pallas_call | solution.py:82
  74.2 25.3 %shard_map.281 = (bf16[1024,256]{1,0:T(8,128)(2,1)}, bf16[1024,256]{1,0:T(8,128)(2,1)}, bf16[24,128,256]{2,1,0:T(8,128)(2,1)}, bf16[8,128,256]{2,1,0:T(8,128)(2,1)}) custom-call(bf16[1024,256]{1,0:T(8,128)(2,1)} %shard_map.280.agg, bf16[512,256]{1,0:T(8,128)(2,1)} %get-tuple-element.37.w_own, bf16[512,256]{1,0:T(8,128)(2,1)} %get-tuple-element.44.w_peer, ...), custom_call_target="tpu_custom_call" | custom-call | flops 268435456 | bytes 1048576 | tf_op jit(solution)/shard_map/pallas_call | solution.py:287
  99.5 3.7 %shard_map.282.agg = bf16[1024,256]{1,0:T(8,128)(2,1)} custom-call(s32[96]{0:T(128)} %send_ids.6, s32[96]{0:T(128)} %recv_ids.6, s32[1]{0:T(128)S(6)} %copy.32.live, f32[3,8]{1,0:T(4,128)} %gains.7, s32[96,2,128]{2,1,0:T(2,128)} %offsets.6, s32[96,128]{1,0:T(8,128)} %labels.6, f32[2,256]{1,0:T(2,128)} %bias.3, ...), custom_call_target="tpu_custom_call" | custom-call | flops 268435456 | bytes 1048576 | tf_op jit(solution)/shard_map/pallas_call | solution.py:82
  103.2 6.8 %shard_map.283 = (bf16[1024,256]{1,0:T(8,128)(2,1)}, bf16[1024,256]{1,0:T(8,128)(2,1)}, bf16[8,128,256]{2,1,0:T(8,128)(2,1)}) custom-call(bf16[1024,256]{1,0:T(8,128)(2,1)} %shard_map.282.agg, bf16[512,256]{1,0:T(8,128)(2,1)} %get-tuple-element.36.w_own, bf16[512,256]{1,0:T(8,128)(2,1)} %get-tuple-element.43.w_peer, f32[2,256]{1,0:T(2,128)} %gain_own.3, ...), custom_call_target="tpu_custom_call" | custom-call | flops 268435456 | bytes 1048576 | tf_op jit(solution)/shard_map/pallas_call | solution.py:287
  110.0 3.8 %shard_map.284.agg = bf16[1024,256]{1,0:T(8,128)(2,1)} custom-call(s32[24]{0:T(128)} %send_ids.7, s32[24]{0:T(128)} %recv_ids.7, s32[1]{0:T(128)S(6)} %copy.33.live, f32[3,8]{1,0:T(4,128)} %gains.7, s32[24,2,128]{2,1,0:T(2,128)} %offsets.7, s32[24,128]{1,0:T(8,128)} %labels.7, f32[1,256]{1,0:T(1,128)} %bitcast.34, ...), custom_call_target="tpu_custom_call" | custom-call | flops 268435456 | bytes 1048576 | tf_op jit(solution)/shard_map/pallas_call | solution.py:82
  113.8 5.3 %shard_map.285 = bf16[1024,256]{1,0:T(8,128)(2,1)} custom-call(bf16[1024,256]{1,0:T(8,128)(2,1)} %shard_map.284.agg, bf16[512,256]{1,0:T(8,128)(2,1)} %get-tuple-element.46.w_own, bf16[512,256]{1,0:T(8,128)(2,1)} %get-tuple-element.42.w_peer, f32[1,256]{1,0:T(1,128)} %bitcast.36), custom_call_target="tpu_custom_call" | custom-call | flops 268435456 | bytes 1048576 | tf_op jit(solution)/shard_map/pallas_call | solution.py:318
  119.1 0.0 copy-start.5
  119.1 19.0 %all-to-all-start.1 = ((bf16[128,8,256]{2,1,0:T(8,128)(2,1)}), bf16[128,8,256]{2,1,0:T(8,128)(2,1)S(1)}, u32[]{:S(2)}, u32[]{:S(2)}) async-start(bf16[128,8,256]{2,1,0:T(8,128)(2,1)} %bitcast.31), calls=%async_computation.1 | async-start | bytes 1048576 | tf_op jit(solution)/shard_map/all_to_all | solution.py:426
  138.1 20.5 %all-to-all-done.1 = bf16[128,8,256]{2,1,0:T(8,128)(2,1)S(1)} async-done(((bf16[128,8,256]{2,1,0:T(8,128)(2,1)}), bf16[128,8,256]{2,1,0:T(8,128)(2,1)S(1)}, u32[]{:S(2)}, u32[]{:S(2)}) %all-to-all-start.1) | async-done | bytes 524320 | tf_op jit(solution)/shard_map/all_to_all | solution.py:426
  158.5 0.8 copy-done.2
  159.3 2.9 %shard_map.286 = bf16[1024,256]{1,0:T(8,128)(2,1)} custom-call(s32[1,1024]{1,0:T(1,128)} %order.3, bf16[1024,256]{1,0:T(8,128)(2,1)} %bitcast.28, bf16[1024,256]{1,0:T(8,128)(2,1)} %grid.3), custom_call_target="tpu_custom_call" | custom-call | flops 268435456 | bytes 1048576 | tf_op jit(solution)/shard_map/pallas_call | solution.py:360
  162.2 0.0 copy-done.5
  162.2 0.8 copy.34
  (2 shorter events, 0.0 us)
Async XLA Ops:
  0.6 18.8 %copy-start = (bf16[2,3,512,256]{3,2,1,0:T(8,128)(2,1)S(1)}, bf16[2,3,512,256]{3,2,1,0:T(8,128)(2,1)}, u32[]{:S(2)}) copy-start(bf16[2,3,512,256]{3,2,1,0:T(8,128)(2,1)} %param.48) | copy-start | bytes 4718596
  4.0 35.6 %all-to-all-start = ((bf16[128,8,256]{2,1,0:T(8,128)(2,1)}), bf16[128,8,256]{2,1,0:T(8,128)(2,1)S(1)}, u32[]{:S(2)}, u32[]{:S(2)}) async-start(bf16[128,8,256]{2,1,0:T(8,128)(2,1)} %bitcast.29), calls=%async_computation | async-start | bytes 1048576 | tf_op jit(solution)/shard_map/all_to_all | solution.py:393
  22.6 7.2 %copy-start.1 = (bf16[3,512,256]{2,1,0:T(8,128)(2,1)S(1)}, bf16[3,512,256]{2,1,0:T(8,128)(2,1)}, u32[]{:S(2)}) copy-start(bf16[3,512,256]{2,1,0:T(8,128)(2,1)} %dec.3) | copy-start | bytes 2359300
  30.7 1.9 %copy-start.4 = (bf16[4,512,256]{2,1,0:T(8,128)(2,1)S(1)}, bf16[4,512,256]{2,1,0:T(8,128)(2,1)}, u32[]{:S(2)}) copy-start(bf16[4,512,256]{2,1,0:T(8,128)(2,1)} %get-tuple-element.21) | copy-start | bytes 3145732
  39.6 0.8 copy-start.3
  119.1 43.2 %copy-start.5 = (bf16[1024,256]{1,0:T(8,128)(2,1)S(1)}, bf16[1024,256]{1,0:T(8,128)(2,1)}, u32[]{:S(2)}) copy-start(bf16[1024,256]{1,0:T(8,128)(2,1)} %get-tuple-element.52) | copy-start | bytes 1572868
  119.1 39.4 %all-to-all-start.1 = ((bf16[128,8,256]{2,1,0:T(8,128)(2,1)}), bf16[128,8,256]{2,1,0:T(8,128)(2,1)S(1)}, u32[]{:S(2)}, u32[]{:S(2)}) async-start(bf16[128,8,256]{2,1,0:T(8,128)(2,1)} %bitcast.31), calls=%async_computation.1 | async-start | bytes 1048576 | tf_op jit(solution)/shard_map/all_to_all | solution.py:426
  158.5 0.8 copy-start.2

commit v3 on v2

--- a/solution.py
+++ b/solution.py
@@ -141,49 +141,6 @@
     return mine, (mixed_peer - average) * scale * gain_peer
 
 
-def setup_kernel(enc, first, second, dec, enc_gain, mesh_gain, own, outer, enc_gain_peer, mesh_gain_peer, peer, take, *sems):
-    feat = lax.axis_index("feat")
-    partner = {"feat": 1 - feat}
-    meet([partner])
-    send_sems, recv_sems = sems
-    pieces = own.shape[0] // PIECE
-    moves = [(own.at[pl.ds(c * PIECE, PIECE)], peer.at[pl.ds(c * PIECE, PIECE)]) for c in range(pieces)]
-    moves += [(enc.at[2], outer.at[0]), (first.at[0, 2], outer.at[1]), (second.at[0, 2], outer.at[2]), (dec.at[2], outer.at[3])]
-    moves += [(enc_gain, enc_gain_peer), (mesh_gain, mesh_gain_peer)]
-    copies = [remote(s, t, send_sems.at[i], recv_sems.at[i], partner) for i, (s, t) in enumerate(moves)]
-    for copy in copies:
-        copy.start()
-    weight = ordered(enc.at[1], feat)
-    for c in range(pieces):
-        copies[c].wait_recv()
-        rows = rows_of(c)
-        put(take, c, dot(jnp.concatenate([own[rows, :], peer[rows, :]], axis=1), weight))
-    for copy in copies[pieces:]:
-        copy.wait_recv()
-    for copy in copies:
-        copy.wait_send()
-
-
-def setup(enc, mesh_w, dec, enc_gain, mesh_gain, own):
-    rows, width = own.shape
-    count = rows // PIECE + 6
-    shape = jax.ShapeDtypeStruct
-    return call(
-        setup_kernel,
-        [VMEM] * 7,
-        [
-            shape((4, D, width), BF16),
-            shape((1, width), F32),
-            shape((ROUNDS, width), F32),
-            shape((rows, width), BF16),
-            shape((rows // BLOCK, BLOCK, width), BF16),
-        ],
-        [DMA((count,)), DMA((count,))],
-        collective_id=0,
-        has_side_effects=True,
-    )(enc, mesh_w[0:1], mesh_w[1:2], dec, enc_gain, mesh_gain, own)
-
-
 def exchange(own, peer, send_sems, recv_sems, partner):
     return [
         remote(own.at[pl.ds(c * PIECE, PIECE)], peer.at[pl.ds(c * PIECE, PIECE)], send_sems.at[c], recv_sems.at[c], partner)
@@ -191,39 +148,7 @@
     ]
 
 
-def grid_kernel(own, enc, dec, sides, takes, peer, send_sems, recv_sems):
-    feat = lax.axis_index("feat")
-    partner = {"feat": 1 - feat}
-    meet([partner])
-    copies = exchange(own, peer, send_sems, recv_sems, partner)
-    for copy in copies:
-        copy.start()
-    first, second = ordered(enc.at[0], feat), ordered(dec.at[1], feat)
-    for c, copy in enumerate(copies):
-        copy.wait_recv()
-        rows = rows_of(c)
-        both = jnp.concatenate([own[rows, :], peer[rows, :]], axis=1)
-        put(sides, c, dot(both, first))
-        put(takes, c, dot(both, second))
-    for copy in copies:
-        copy.wait_send()
-
-
-def grid_sides(own, enc, dec):
-    rows, width = own.shape
-    shape = jax.ShapeDtypeStruct((rows // BLOCK, BLOCK, width), BF16)
-    count = rows // PIECE
-    return call(
-        grid_kernel,
-        [VMEM] * 3,
-        [shape, shape],
-        [pltpu.VMEM((rows, width), BF16), DMA((count,)), DMA((count,))],
-        collective_id=1,
-        has_side_effects=True,
-    )(own, enc, dec)
-
-
-def refresh_kernel(near, stage, gain_row, agg, w_own, w_peer, gain_own, gain_peer, mesh_own, mesh_peer, following, new_own, new_peer, sent, *refs):
+def refresh_kernel(near, stage, own_at, next_at, gain_row, agg, w_own, w_peer, gain_own, gain_peer, mesh_own, mesh_peer, following, new_own, new_peer, sent, *refs):
     feat = lax.axis_index("feat")
     partner = {"feat": 1 - feat}
     if near:
@@ -248,7 +173,7 @@
             here = sent.at[pl.ds(blocks + c * per, per)]
             outgoing.append(remote(here, sent.at[pl.ds(c * per, per)], up_send.at[c], up_recv.at[c], after))
             outgoing.append(remote(here, sent.at[pl.ds(2 * blocks + c * per, per)], down_send.at[c], down_recv.at[c], before))
-    mine, theirs = ordered(w_own, feat), ordered(w_peer, feat)
+    mine, theirs = ordered(w_own.at[own_at], feat), ordered(w_peer.at[stage], feat)
     for c, copy in enumerate(copies):
         copy.wait_recv()
         rows = rows_of(c)
@@ -261,12 +186,12 @@
         new_own[rows, :] = own
         new_peer[rows, :] = other
         both = jnp.concatenate([own, other], axis=1)
-        put(sent.at[pl.ds(shift, blocks)], c, dot(both, ordered(following.at[0], feat)))
+        put(sent.at[pl.ds(shift, blocks)], c, dot(both, ordered(following.at[next_at + (0,)], feat)))
         if near:
             if c:
                 outgoing[2 * c - 2].start()
                 outgoing[2 * c - 1].start()
-            put(take, c, dot(both, ordered(following.at[1], feat)))
+            put(take, c, dot(both, ordered(following.at[next_at + (1,)], feat)))
     for copy in outgoing[2 * pieces - 2 :]:
         copy.start()
     for copy in outgoing:
@@ -275,7 +200,7 @@
         copy.wait_send()
 
 
-def refresh(stage, near, agg, w_own, w_peer, gain_own, gain_peer, gain_row, mesh_own, mesh_peer, following):
+def refresh(stage, near, own_at, next_at, agg, w_own, w_peer, gain_own, gain_peer, gain_row, mesh_own, mesh_peer, following):
     rows, width = agg.shape
     blocks, count = rows // BLOCK, rows // PIECE
     shape = jax.ShapeDtypeStruct
@@ -285,7 +210,7 @@
         outs.append(shape((blocks, BLOCK, width), BF16))
         scratch += [DMA((count,))] * 4
     return call(
-        functools.partial(refresh_kernel, near, stage, gain_row),
+        functools.partial(refresh_kernel, near, stage, own_at, next_at, gain_row),
         [VMEM] * 8,
         outs,
         scratch,
@@ -294,70 +219,215 @@
     )(agg, w_own, w_peer, gain_own, gain_peer, mesh_own, mesh_peer, following)
 
 
-def update_kernel(agg, w_own, w_peer, gain_own, out, peer, send_sems, recv_sems):
-    feat = lax.axis_index("feat")
+def extents(size):
+    return (8, 4, 4) if size == 128 else (1, 2, size // 2)
+
+
+def axis_peers(node, size):
+    z, x, y = extents(size)
+    at = (node // (x * y), (node // y) % x, node % y)
+    index = lambda p: (p[0] * x + p[1]) * y + p[2]
+    peers = []
+    for axis, extent in enumerate((z, x, y)):
+        line = []
+        for step in range(1, extent):
+            spot = list(at)
+            spot[axis] = lax.rem(at[axis] + step, extent)
+            line.append({"nodes": index(spot)})
+        peers.append(line)
+    return peers
+
+
+def signal_all(semaphore, partners):
+    for partner in partners:
+        pl.semaphore_signal(semaphore, inc=1, device_id=partner, device_id_type=MESH_ID)
+
+
+def send_all(node, size, source, target, send_sem, recv_sem):
+    z, x, y = extents(size)
+
+    def send(i, carry):
+        j = size - i
+        to_z = lax.rem(node // (x * y) + lax.rem(j, z), z)
+        to_x = lax.rem((node // y) % x + lax.rem(j // z, x), x)
+        to_y = lax.rem(node % y + j // (z * x), y)
+        to = (to_z * x + to_x) * y + to_y
+        remote(source.at[to], target.at[node], send_sem, recv_sem, {"nodes": to}).start()
+        return carry
+
+    lax.fori_loop(1, size, send, 0)
+    target[pl.ds(node, 1)] = source[pl.ds(node, 1)]
+
+
+def drain(size, source, target, send_sem, recv_sem, partner):
+    rest = pl.ds(0, size - 1)
+    return remote(source.at[rest], target.at[rest], send_sem, recv_sem, partner)
+
+
+def flat(ref, c):
+    per = PIECE // ref.shape[1]
+    return ref[pl.ds(c * per, per)].astype(F32).reshape(PIECE, ref.shape[2]).astype(BF16)
+
+
+def put_split(ref, c, value):
+    per = PIECE // ref.shape[1]
+    ref[pl.ds(c * per, per)] = value.reshape(per, ref.shape[1], ref.shape[2]).astype(BF16)
+
+
+def start_kernel(
+    order, grid, own, enc, mesh_w, dec, enc_gain, mesh_gain,
+    sides, takes, take, peer, outer, enc_gain_peer, mesh_gain_peer,
+    picked, arrived, other, send_sems, recv_sems, grid_sends, grid_recvs, send_sem, recv_sem, x_sem, y_sem,
+):
+    feat, node, size = lax.axis_index("feat"), lax.axis_index("nodes"), lax.axis_size("nodes")
     partner = {"feat": 1 - feat}
-    meet([partner])
+    line_z, line_x, line_y = axis_peers(node, size)
+    barrier = pltpu.get_barrier_semaphore()
+    first = [partner] + line_z + line_x + line_y
+    signal_all(barrier, first)
+    rows = grid.shape[0]
+    pieces = rows // PIECE
+    spot = lax.broadcasted_iota(jnp.int32, (rows, BLOCK), 0)
+
+    def choose(c):
+        parts = []
+        for h in range(PIECE // BLOCK):
+            here = pl.ds(c * PIECE + h * BLOCK, BLOCK)
+            hot = jnp.where(spot == order[:, here], 1.0, 0.0).astype(BF16)
+            parts.append(dot(hot, grid[...], ((0,), (0,))))
+        put_split(picked, c, jnp.concatenate(parts, axis=0))
+
+    moves = [(own.at[pl.ds(c * PIECE, PIECE)], peer.at[pl.ds(c * PIECE, PIECE)]) for c in range(pieces)]
+    moves += [(enc.at[2], outer.at[0])] + [(mesh_w.at[r, 2], outer.at[1 + r]) for r in range(ROUNDS)]
+    moves += [(dec.at[2], outer.at[1 + ROUNDS]), (enc_gain, enc_gain_peer), (mesh_gain, mesh_gain_peer)]
+    copies = [remote(s, t, send_sems.at[i], recv_sems.at[i], partner) for i, (s, t) in enumerate(moves)]
+
+    for c in range(pieces):
+        choose(c)
+        if c == pieces // 2 - 1:
+            pl.semaphore_wait(barrier, len(first))
+            signal_all(x_sem, line_x)
+            for copy in copies:
+                copy.start()
+        if c == pieces - 2:
+            pl.semaphore_wait(x_sem, len(line_x))
+            signal_all(y_sem, line_y)
+    pl.semaphore_wait(y_sem, len(line_y))
+    send_all(node, size, picked, arrived, send_sem, recv_sem)
+    weight = ordered(enc.at[1], feat)
+    for c in range(pieces):
+        copies[c].wait_recv()
+        here = rows_of(c)
+        put(take, c, dot(jnp.concatenate([own[here, :], peer[here, :]], axis=1), weight))
+    for copy in copies[pieces:]:
+        copy.wait_recv()
+    for copy in copies:
+        copy.wait_send()
+    whole = drain(size, picked, arrived, send_sem, recv_sem, partner)
+    whole.wait_recv()
+    per = PIECE // arrived.shape[1]
+    passes = [
+        remote(arrived.at[pl.ds(c * per, per)], other.at[pl.ds(c * per, per)], grid_sends.at[c], grid_recvs.at[c], partner)
+        for c in range(pieces)
+    ]
+    for copy in passes:
+        copy.start()
+    first_w, second_w = ordered(enc.at[0], feat), ordered(dec.at[1], feat)
+    for c, copy in enumerate(passes):
+        copy.wait_recv()
+        both = jnp.concatenate([flat(arrived, c), flat(other, c)], axis=1)
+        put(sides, c, dot(both, first_w))
+        put(takes, c, dot(both, second_w))
+    for copy in passes:
+        copy.wait_send()
+    whole.wait_send()
+
+
+def start(order, grid, own, enc, mesh_w, dec, enc_gain, mesh_gain):
+    rows, width = own.shape
+    size = lax.axis_size("nodes")
+    count, pieces = rows // PIECE + 4 + ROUNDS, rows // PIECE
+    shape = jax.ShapeDtypeStruct
+    blocked = shape((rows // BLOCK, BLOCK, width), BF16)
+    split = pltpu.VMEM((size, rows // size, width), BF16)
+    regular = pltpu.SemaphoreType.REGULAR
+    return call(
+        start_kernel,
+        [VMEM] * 8,
+        [
+            blocked,
+            blocked,
+            blocked,
+            shape((rows, width), BF16),
+            shape((2 + ROUNDS, D, width), BF16),
+            shape((1, width), F32),
+            shape((ROUNDS, width), F32),
+        ],
+        [split] * 3 + [DMA((count,))] * 2 + [DMA((pieces,))] * 2 + [DMA] * 2 + [regular] * 2,
+        collective_id=0,
+        has_side_effects=True,
+    )(order, grid, own, enc, mesh_w, dec, enc_gain, mesh_gain)
+
+
+def finish_kernel(
+    agg, dec, outer, gain, order, grid, out,
+    peer, update, returned, hot, landed, send_sems, recv_sems, send_sem, recv_sem, x_sem, y_sem,
+):
+    feat, node, size = lax.axis_index("feat"), lax.axis_index("nodes"), lax.axis_size("nodes")
+    partner = {"feat": 1 - feat}
+    line_z, line_x, line_y = axis_peers(node, size)
+    barrier = pltpu.get_barrier_semaphore()
+    first = [partner] + line_z + line_x + line_y
+    signal_all(barrier, first)
+    pl.semaphore_wait(barrier, len(first))
     copies = exchange(agg, peer, send_sems, recv_sems, partner)
     for copy in copies:
         copy.start()
-    mine, theirs = ordered(w_own, feat), ordered(w_peer, feat)
+    signal_all(x_sem, line_x)
+    mine, theirs = ordered(dec.at[2], feat), ordered(outer.at[1 + ROUNDS], feat)
+    pieces = len(copies)
     for c, copy in enumerate(copies):
         copy.wait_recv()
-        rows = rows_of(c)
-        both = jnp.concatenate([agg[rows, :], peer[rows, :]], axis=1)
-        own, _ = normed(dot(both, mine), dot(both, theirs), gain_own[...], None)
-        out[rows, :] = own.astype(BF16)
+        here = rows_of(c)
+        both = jnp.concatenate([agg[here, :], peer[here, :]], axis=1)
+        fresh, _ = normed(dot(both, mine), dot(both, theirs), gain[...], None)
+        put_split(update, c, fresh)
+        if c == pieces // 2 - 1:
+            pl.semaphore_wait(x_sem, len(line_x))
+            signal_all(y_sem, line_y)
+    pl.semaphore_wait(y_sem, len(line_y))
+    send_all(node, size, update, returned, send_sem, recv_sem)
+    rows = grid.shape[0]
+    for c in range(pieces):
+        spot = lax.broadcasted_iota(jnp.int32, (PIECE, rows), 0) + c * PIECE
+        hot[c * PIECE : (c + 1) * PIECE, :] = jnp.where(spot == order[...], 1.0, 0.0).astype(BF16)
     for copy in copies:
         copy.wait_send()
-
-
-def update_of(agg, w_own, w_peer, gain_own):
+    whole = drain(size, update, returned, send_sem, recv_sem, partner)
+    whole.wait_recv()
+    for c in range(pieces):
+        landed[c * PIECE : (c + 1) * PIECE, :] = flat(returned, c)
+    for c in range(pieces):
+        here = slice(c * PIECE, (c + 1) * PIECE)
+        out[here, :] = (grid[here, :].astype(F32) + dot(hot[here, :], landed[...])).astype(BF16)
+    whole.wait_send()
+
+
+def finish(agg, dec, outer, gain, order, grid):
     rows, width = agg.shape
-    count = rows // PIECE
+    size = lax.axis_size("nodes")
+    pieces = rows // PIECE
+    split = pltpu.VMEM((size, rows // size, width), BF16)
+    regular = pltpu.SemaphoreType.REGULAR
     return call(
-        update_kernel,
-        [VMEM] * 4,
+        finish_kernel,
+        [VMEM] * 6,
         jax.ShapeDtypeStruct(agg.shape, BF16),
-        [pltpu.VMEM((rows, width), BF16), DMA((count,)), DMA((count,))],
+        [pltpu.VMEM((rows, width), BF16), split, split, pltpu.VMEM((rows, rows), BF16), pltpu.VMEM((rows, width), BF16)]
+        + [DMA((pieces,))] * 2 + [DMA] * 2 + [regular] * 2,
         collective_id=6,
         has_side_effects=True,
-    )(agg, w_own, w_peer, gain_own)
-
-
-def pick_kernel(order, grid, out):
-    rows = grid.shape[0]
-    spot = lax.broadcasted_iota(jnp.int32, (rows, BLOCK), 0)
-
-    def step(b, carry):
-        here = pl.ds(pl.multiple_of(b * BLOCK, BLOCK), BLOCK)
-        hot = jnp.where(spot == order[:, here], 1.0, 0.0).astype(BF16)
-        out[here, :] = dot(hot, grid[...], ((0,), (0,))).astype(BF16)
-        return carry
-
-    lax.fori_loop(0, rows // BLOCK, step, 0, unroll=2)
-
-
-def pick(order, grid):
-    return call(pick_kernel, [VMEM] * 2, jax.ShapeDtypeStruct(grid.shape, BF16))(order, grid)
-
-
-def place_kernel(order, returned, grid, out):
-    rows = grid.shape[0]
-
-    def step(b, carry):
-        start = pl.multiple_of(b * PIECE, PIECE)
-        here = pl.ds(start, PIECE)
-        spot = lax.broadcasted_iota(jnp.int32, (PIECE, rows), 0) + start
-        hot = jnp.where(spot == order[...], 1.0, 0.0).astype(BF16)
-        out[here, :] = (grid[here, :].astype(F32) + dot(hot, returned[...])).astype(BF16)
-        return carry
-
-    lax.fori_loop(0, rows // PIECE, step, 0, unroll=2)
-
-
-def place(order, returned, grid):
-    return call(place_kernel, [VMEM] * 3, jax.ShapeDtypeStruct(grid.shape, BF16))(order, returned, grid)
+    )(agg, dec, outer, gain, order, grid)
 
 
 def local(
@@ -390,19 +460,16 @@
     dec_bias,
     dec_gain,
 ):
-    arrived = lax.all_to_all(pick(grid_order, grid_latent), "nodes", split_axis=0, concat_axis=0, tiled=True)
-    outer_peer, enc_gain_peer, mesh_gain_peer, mesh_peer, mesh_take = setup(
-        enc_weights, mesh_weights, dec_weights, enc_gain[None, :], mesh_gain, mesh_latent
-    )
-    mesh_own = mesh_latent
-    grid_send, grid_take = grid_sides(arrived, enc_weights, dec_weights)
+    grid_send, grid_take, mesh_take, mesh_peer, outer, enc_gain_peer, mesh_gain_peer = start(
+        grid_order, grid_latent, mesh_latent, enc_weights, mesh_weights, dec_weights, enc_gain[None, :], mesh_gain
+    )
     agg = edge_sum(
         grid_send, mesh_take, enc_bias[None, :], 0, class_gain, 0,
         enc_send_block, enc_recv_block, enc_offsets, enc_classes, enc_live, 8,
     )
     mesh_own, mesh_peer, nearby, taking = refresh(
-        0, True, agg, enc_weights[2], outer_peer[0], enc_gain[None, :], enc_gain_peer, 0,
-        mesh_own, mesh_peer, mesh_weights[0, 0:2],
+        0, True, (2,), (0,), agg, enc_weights, outer, enc_gain[None, :], enc_gain_peer, 0,
+        mesh_latent, mesh_peer, mesh_weights,
     )
     for index in range(ROUNDS):
         agg = edge_sum(
@@ -410,10 +477,9 @@
             mesh_send_block, mesh_recv_block, mesh_offsets, mesh_classes, mesh_live, 16,
         )
         last = index == ROUNDS - 1
-        following = dec_weights[0:1] if last else mesh_weights[index + 1, 0:2]
         mesh_own, mesh_peer, *sides = refresh(
-            index + 1, not last, agg, mesh_weights[index, 2], outer_peer[index + 1], mesh_gain, mesh_gain_peer, index,
-            mesh_own, mesh_peer, following,
+            index + 1, not last, (index, 2), () if last else (index + 1,), agg, mesh_weights, outer,
+            mesh_gain, mesh_gain_peer, index, mesh_own, mesh_peer, dec_weights if last else mesh_weights,
         )
         if not last:
             nearby, taking = sides
@@ -422,9 +488,7 @@
         dec_send, grid_take, dec_bias[None, :], 0, class_gain, 2,
         dec_send_block, dec_recv_block, dec_offsets, dec_classes, dec_live, 12,
     )
-    update = update_of(agg, dec_weights[2], outer_peer[3], dec_gain[None, :])
-    returned = lax.all_to_all(update, "nodes", split_axis=0, concat_axis=0, tiled=True)
-    return (place(grid_order, returned, grid_latent), mesh_own)
+    return (finish(agg, dec_weights, outer, dec_gain[None, :], grid_order, grid_latent), mesh_own)
 
 
 def solution(mesh):

time: 165 us -> 146 us (0.88)
  Pallas kernels: 92.1 us -> 139 us
  starting transfers between devices: 34.4 us -> 0 us
  waiting for transfers between devices: 25.4 us -> 0 us
  local copies, waits for them, and re-layouts: 8.49 us -> 2.67 us
    pallas_call x8 -> x5, Pallas kernels: 78.2 us -> 119 us  [the longest x3 53.1 us: refresh(): call(functools.partial(refresh_kernel, near, stage, own_at, next_at, gain...]
    all_to_all x2 -> x0, starting transfers between devices: 34.4 us -> none  [the longest x1 19 us: local(): lax.all_to_all(update, 'nodes', split_axis=0, concat_axis=0, tiled=True)]
    all_to_all x2 -> x0, waiting for transfers between devices: 25.4 us -> none  [the longest x1 20.5 us: local(): lax.all_to_all(update, 'nodes', split_axis=0, concat_axis=0, tiled=True)]
    pallas_call x4, Pallas kernels: 13.8 us -> 20.8 us  [edge_sum(): call(functools.partial(edge_kernel, unroll, gain_row, bias_row), [SMEM] *...]
    squeeze x4 -> x0, local copies, waits for them, and re-layouts: 4.84 us -> none  [the longest x2 2.94 us: local(): update = update_of(agg, dec_weights[2], outer_peer[3], dec_gain[None, :])]
  transfers between devices with their start and end apart: 2 -> 0, of which waited for: 2 -> 0; matrix products, arithmetic and copies ran while one was open for 4% -> 0% of each run, Pallas kernels for 4% -> 0%
where the time goes in v3:
time: 146 us; the launch traced here: 145 us
  Pallas kernels  139 us (95%)
  local copies, waits for them, and re-layouts  2.67 us (2%)
  between operations  2.61 us (2%)
    pallas_call x3, Pallas kernels, refresh(): call(functools.partial(refresh_kernel, near, stage, own_at, next_at, gain...  53.1 us
    pallas_call x1, Pallas kernels, finish(): call(finish_kernel, [VMEM] * 6, jax.ShapeDtypeStruct(agg.shape, BF16), [p...  33.8 us
    pallas_call x1, Pallas kernels, start(): call(start_kernel, [VMEM] * 8, [blocked, blocked, blocked, shape((rows, w...  31.6 us
    pallas_call x4, Pallas kernels, edge_sum(): call(functools.partial(edge_kernel, unroll, gain_row, bias_row), [SMEM] *...  20.8 us

profile of v3, /device:TPU:2, one launch (start us, length us, event | category | flops | bytes accessed | tf_op | source)
XLA Modules:
  0.0 144.6 jit_solution(2473668618529978328)
XLA Ops:
  0.6 31.6 %shard_map.275 = (bf16[8,128,256]{2,1,0:T(8,128)(2,1)}, bf16[8,128,256]{2,1,0:T(8,128)(2,1)}, bf16[8,128,256]{2,1,0:T(8,128)(2,1)}, bf16[1024,256]{1,0:T(8,128)(...) custom-call(s32[1,1024]{1,0:T(1,128)} %order.3, bf16[1024,256]{1,0:T(8,128)(2,1)} %grid.3, ...), custom_call_target="tpu_custom_call" | custom-call | flops 268435456 | bytes 1048576 | tf_op jit(solution)/shard_map/pallas_call | solution.py:354
  32.9 2.8 %shard_map.276.agg = bf16[1024,256]{1,0:T(8,128)(2,1)} custom-call(s32[16]{0:T(128)} %send_ids.4, s32[16]{0:T(128)} %recv_ids.4, s32[1]{0:T(128)S(6)} %copy.32.live, f32[3,8]{1,0:T(4,128)} %gains.7, s32[16,2,128]{2,1,0:T(2,128)} %offsets.4, s32[16,128]{1,0:T(8,128)} %labels.4, f32[1,256]{1,0:T(1,128)} %bitcast.8, ...), custom_call_target="tpu_custom_call" | custom-call | flops 268435456 | bytes 1048576 | tf_op jit(solution)/shard_map/pallas_call | solution.py:82
  35.7 23.3 %shard_map.277 = (bf16[1024,256]{1,0:T(8,128)(2,1)}, bf16[1024,256]{1,0:T(8,128)(2,1)}, bf16[24,128,256]{2,1,0:T(8,128)(2,1)}, bf16[8,128,256]{2,1,0:T(8,128)(2,1)}) custom-call(bf16[1024,256]{1,0:T(8,128)(2,1)} %shard_map.276.agg, bf16[3,512,256]{2,1,0:T(8,128)(2,1)} %w_own.3, bf16[4,512,256]{2,1,0:T(8,128)(2,1)} %get-tuple-element.21.w_peer.outer, ...), custom_call_target="tpu_custom_call" | custom-call | flops 268435456 | bytes 1048576 | tf_op jit(solution)/shard_map/pallas_call | solution.py:212
  59.6 7.4 %shard_map.278.agg = bf16[1024,256]{1,0:T(8,128)(2,1)} custom-call(s32[96]{0:T(128)} %send_ids.6, s32[96]{0:T(128)} %recv_ids.6, s32[1]{0:T(128)S(6)} %copy.33.live, f32[3,8]{1,0:T(4,128)} %gains.7, s32[96,2,128]{2,1,0:T(2,128)} %offsets.6, s32[96,128]{1,0:T(8,128)} %labels.6, f32[2,256]{1,0:T(2,128)} %bias.3, ...), custom_call_target="tpu_custom_call" | custom-call | flops 268435456 | bytes 1048576 | tf_op jit(solution)/shard_map/pallas_call | solution.py:82
  67.1 22.2 %shard_map.279 = (bf16[1024,256]{1,0:T(8,128)(2,1)}, bf16[1024,256]{1,0:T(8,128)(2,1)}, bf16[24,128,256]{2,1,0:T(8,128)(2,1)}, bf16[8,128,256]{2,1,0:T(8,128)(2,1)}) custom-call(bf16[1024,256]{1,0:T(8,128)(2,1)} %shard_map.278.agg, bf16[2,3,512,256]{3,2,1,0:T(8,128)(2,1)} %w_own.5, bf16[4,512,256]{2,1,0:T(8,128)(2,1)} %get-tuple-element.21.w_peer.outer, ...), custom_call_target="tpu_custom_call" | custom-call | flops 268435456 | bytes 1048576 | tf_op jit(solution)/shard_map/pallas_call | solution.py:212
  89.3 7.6 %shard_map.280.agg = bf16[1024,256]{1,0:T(8,128)(2,1)} custom-call(s32[96]{0:T(128)} %send_ids.6, s32[96]{0:T(128)} %recv_ids.6, s32[1]{0:T(128)S(6)} %copy.33.live, f32[3,8]{1,0:T(4,128)} %gains.7, s32[96,2,128]{2,1,0:T(2,128)} %offsets.6, s32[96,128]{1,0:T(8,128)} %labels.6, f32[2,256]{1,0:T(2,128)} %bias.3, ...), custom_call_target="tpu_custom_call" | custom-call | flops 268435456 | bytes 1048576 | tf_op jit(solution)/shard_map/pallas_call | solution.py:82
  96.9 7.6 %shard_map.281 = (bf16[1024,256]{1,0:T(8,128)(2,1)}, bf16[1024,256]{1,0:T(8,128)(2,1)}, bf16[8,128,256]{2,1,0:T(8,128)(2,1)}) custom-call(bf16[1024,256]{1,0:T(8,128)(2,1)} %shard_map.280.agg, bf16[2,3,512,256]{3,2,1,0:T(8,128)(2,1)} %w_own.5, bf16[4,512,256]{2,1,0:T(8,128)(2,1)} %get-tuple-element.21.w_peer.outer, f32[2,256]{1,0:T(2,128)} %gain_own.3, ...), custom_call_target="tpu_custom_call" | custom-call | flops 268435456 | bytes 1048576 | tf_op jit(solution)/shard_map/pallas_call | solution.py:212
  105.1 3.0 %shard_map.282.agg = bf16[1024,256]{1,0:T(8,128)(2,1)} custom-call(s32[24]{0:T(128)} %send_ids.7, s32[24]{0:T(128)} %recv_ids.7, s32[1]{0:T(128)S(6)} %copy.34.live, f32[3,8]{1,0:T(4,128)} %gains.7, s32[24,2,128]{2,1,0:T(2,128)} %offsets.7, s32[24,128]{1,0:T(8,128)} %labels.7, f32[1,256]{1,0:T(1,128)} %bitcast.7, ...), custom_call_target="tpu_custom_call" | custom-call | flops 268435456 | bytes 1048576 | tf_op jit(solution)/shard_map/pallas_call | solution.py:82
  108.1 0.0 copy-start
  108.1 33.8 %shard_map.283 = bf16[1024,256]{1,0:T(8,128)(2,1)} custom-call(bf16[1024,256]{1,0:T(8,128)(2,1)} %shard_map.282.agg, bf16[3,512,256]{2,1,0:T(8,128)(2,1)} %dec.3, bf16[4,512,256]{2,1,0:T(8,128)(2,1)} %get-tuple-element.21.w_peer.outer, f32[1,256]{1,0:T(1,128)} %bitcast.6, s32[1,1024]{1,0:T(1,128)} %order.3, bf16[1024,256]{1,0:T(8,128)(2,1)} %grid.3), custom_call_target="tpu_custom_call" | custom-call | flops 268435456 | bytes 1048576 | tf_op jit(solution)/shard_map/pallas_call | solution.py:422
  141.9 1.9 %copy.35 = bf16[1024,256]{1,0:T(8,128)(2,1)} copy(bf16[1024,256]{1,0:T(8,128)(2,1)} %shard_map.283) | data formatting | bytes 1048576
  143.8 0.0 copy-done
  143.8 0.8 copy.36
Async XLA Ops:
  108.1 35.7 %copy-start = (bf16[1024,256]{1,0:T(8,128)(2,1)S(1)}, bf16[1024,256]{1,0:T(8,128)(2,1)}, u32[]{:S(2)}) copy-start(bf16[1024,256]{1,0:T(8,128)(2,1)} %get-tuple-element.39) | copy-start | bytes 1572868

commit v4 on v3

--- a/solution.py
+++ b/solution.py
@@ -17,17 +17,20 @@
 
 VMEM = pl.BlockSpec(memory_space=pltpu.VMEM)
 SMEM = pl.BlockSpec(memory_space=pltpu.SMEM)
-
-
-def call(kernel, ins, outs, scratch=(), flops=1 << 28, **params):
+HBM = pl.BlockSpec(memory_space=pltpu.HBM)
+LIMIT = 20 << 20
+START_LIMIT = None
+
+
+def call(kernel, ins, outs, scratch=(), flops=1 << 28, out_specs=None, limit=LIMIT, **params):
     return pl.pallas_call(
         kernel,
         in_specs=ins,
-        out_specs=[VMEM] * len(outs) if isinstance(outs, (list, tuple)) else VMEM,
+        out_specs=out_specs or ([VMEM] * len(outs) if isinstance(outs, (list, tuple)) else VMEM),
         out_shape=outs,
         scratch_shapes=list(scratch),
         cost_estimate=pl.CostEstimate(flops=flops, bytes_accessed=1 << 20, transcendentals=0),
-        compiler_params=pltpu.CompilerParams(**params),
+        compiler_params=pltpu.CompilerParams(vmem_limit_bytes=limit, **params),
     )
 
 
@@ -35,7 +38,14 @@
     return lax.dot_general(a, b, (dims, ((), ())), preferred_element_type=F32)
 
 
-def edge_kernel(unroll, gain_row, bias_row, send_ids, recv_ids, live, gains, offsets, labels, bias, sender, receiver, out, total, high, low):
+def edge_kernel(unroll, gain_row, bias_row, send_ids, recv_ids, live, gains, offsets, labels, bias, sender, receiver, *refs):
+    if len(refs) == 7:
+        through, out, through_out, total, high, low, sem = refs
+        passing = pltpu.make_async_copy(through, through_out, sem)
+        passing.start()
+    else:
+        out, total, high, low = refs
+        passing = None
     slots = labels.shape[0]
     blocks = total.shape[0]
     chosen = labels[...]
@@ -74,21 +84,26 @@
     lax.fori_loop(0, (live[0] + unroll - 1) // unroll, turn, 0)
     for b in range(blocks):
         out[b * BLOCK : (b + 1) * BLOCK, :] = total[b].astype(BF16)
-
-
-def edge_sum(sender, receiver, bias, bias_row, gains, gain_row, send_ids, recv_ids, offsets, labels, live, unroll):
+    if passing is not None:
+        passing.wait()
+
+
+def edge_sum(sender, receiver, bias, bias_row, gains, gain_row, send_ids, recv_ids, offsets, labels, live, unroll, through=None):
     slots = labels.shape[0]
     blocks, _, width = receiver.shape
-    return call(
-        functools.partial(edge_kernel, unroll, gain_row, bias_row),
-        [SMEM] * 4 + [VMEM] * 5,
-        jax.ShapeDtypeStruct((blocks * BLOCK, width), BF16),
-        [
-            pltpu.VMEM((blocks, BLOCK, width), F32),
-            pltpu.VMEM((slots, BLOCK), F32),
-            pltpu.VMEM((slots, BLOCK), F32),
-        ],
-    )(send_ids, recv_ids, live, gains, offsets, labels, bias, sender, receiver)
+    result = jax.ShapeDtypeStruct((blocks * BLOCK, width), BF16)
+    scratch = [
+        pltpu.VMEM((blocks, BLOCK, width), F32),
+        pltpu.VMEM((slots, BLOCK), F32),
+        pltpu.VMEM((slots, BLOCK), F32),
+    ]
+    kernel = functools.partial(edge_kernel, unroll, gain_row, bias_row)
+    operands = (send_ids, recv_ids, live, gains, offsets, labels, bias, sender, receiver)
+    specs = [SMEM] * 4 + [VMEM] * 5
+    if through is None:
+        return call(kernel, specs, result, scratch)(*operands)
+    outs = [result, jax.ShapeDtypeStruct(through.shape, through.dtype)]
+    return call(kernel, specs + [VMEM], outs, scratch + [pltpu.SemaphoreType.DMA], out_specs=[VMEM, HBM])(*operands, through)
 
 
 PIECE = 256
@@ -110,8 +125,8 @@
     )
 
 
-def rows_of(c):
-    return pl.ds(pl.multiple_of(c * PIECE, PIECE), PIECE)
+def rows_of(c, piece=PIECE):
+    return pl.ds(pl.multiple_of(c * piece, piece), piece)
 
 
 def ordered(matrix, feat):
@@ -122,7 +137,7 @@
 
 
 def put(out, c, value):
-    per = PIECE // BLOCK
+    per = value.shape[0] // BLOCK
     for i in range(per):
         out[c * per + i] = value[i * BLOCK : (i + 1) * BLOCK, :].astype(BF16)
 
@@ -141,10 +156,11 @@
     return mine, (mixed_peer - average) * scale * gain_peer
 
 
-def exchange(own, peer, send_sems, recv_sems, partner):
+def exchange(own, peer, send_sems, recv_sems, partner, spots=None, piece=PIECE):
+    spots = range(own.shape[0] // piece) if spots is None else spots
     return [
-        remote(own.at[pl.ds(c * PIECE, PIECE)], peer.at[pl.ds(c * PIECE, PIECE)], send_sems.at[c], recv_sems.at[c], partner)
-        for c in range(own.shape[0] // PIECE)
+        remote(own.at[rows_of(s, piece)], peer.at[rows_of(s, piece)], send_sems.at[c], recv_sems.at[c], partner)
+        for c, s in enumerate(spots)
     ]
 
 
@@ -160,11 +176,12 @@
     else:
         peer, send_sems, recv_sems = refs
         meet([partner])
-    copies = exchange(agg, peer, send_sems, recv_sems, partner)
+    piece = BLOCK if near else PIECE
+    copies = exchange(agg, peer, send_sems, recv_sems, partner, piece=piece)
     for copy in copies:
         copy.start()
     pieces = len(copies)
-    per = PIECE // BLOCK
+    per = piece // BLOCK
     blocks = pieces * per
     shift = blocks if near else 0
     outgoing = []
@@ -174,9 +191,13 @@
             outgoing.append(remote(here, sent.at[pl.ds(c * per, per)], up_send.at[c], up_recv.at[c], after))
             outgoing.append(remote(here, sent.at[pl.ds(2 * blocks + c * per, per)], down_send.at[c], down_recv.at[c], before))
     mine, theirs = ordered(w_own.at[own_at], feat), ordered(w_peer.at[stage], feat)
+    if not near:
+        for copy in copies:
+            copy.wait_recv()
     for c, copy in enumerate(copies):
-        copy.wait_recv()
-        rows = rows_of(c)
+        if near:
+            copy.wait_recv()
+        rows = rows_of(c, piece)
         both = jnp.concatenate([agg[rows, :], peer[rows, :]], axis=1)
         own, other = normed(
             dot(both, mine), dot(both, theirs), gain_own[gain_row : gain_row + 1, :], gain_peer[gain_row : gain_row + 1, :]
@@ -188,12 +209,9 @@
         both = jnp.concatenate([own, other], axis=1)
         put(sent.at[pl.ds(shift, blocks)], c, dot(both, ordered(following.at[next_at + (0,)], feat)))
         if near:
-            if c:
-                outgoing[2 * c - 2].start()
-                outgoing[2 * c - 1].start()
             put(take, c, dot(both, ordered(following.at[next_at + (1,)], feat)))
-    for copy in outgoing[2 * pieces - 2 :]:
-        copy.start()
+            outgoing[2 * c].start()
+            outgoing[2 * c + 1].start()
     for copy in outgoing:
         copy.wait_recv()
     for copy in copies + outgoing:
@@ -202,7 +220,7 @@
 
 def refresh(stage, near, own_at, next_at, agg, w_own, w_peer, gain_own, gain_peer, gain_row, mesh_own, mesh_peer, following):
     rows, width = agg.shape
-    blocks, count = rows // BLOCK, rows // PIECE
+    blocks, count = rows // BLOCK, rows // (BLOCK if near else PIECE)
     shape = jax.ShapeDtypeStruct
     outs = [shape((rows, width), BF16)] * 2 + [shape((blocks * (3 if near else 1), BLOCK, width), BF16)]
     scratch = [pltpu.VMEM((rows, width), BF16), DMA((count,)), DMA((count,))]
@@ -259,9 +277,9 @@
     target[pl.ds(node, 1)] = source[pl.ds(node, 1)]
 
 
-def drain(size, source, target, send_sem, recv_sem, partner):
-    rest = pl.ds(0, size - 1)
-    return remote(source.at[rest], target.at[rest], send_sem, recv_sem, partner)
+def drain(ref, count, send_sem, recv_sem, partner):
+    some = ref.at[pl.ds(0, count)]
+    return remote(some, some, send_sem, recv_sem, partner)
 
 
 def flat(ref, c):
@@ -277,7 +295,7 @@
 def start_kernel(
     order, grid, own, enc, mesh_w, dec, enc_gain, mesh_gain,
     sides, takes, take, peer, outer, enc_gain_peer, mesh_gain_peer,
-    picked, arrived, other, send_sems, recv_sems, grid_sends, grid_recvs, send_sem, recv_sem, x_sem, y_sem,
+    picked, arrived, other, mine, near_w, load_sems, send_sems, recv_sems, grid_sends, grid_recvs, send_sem, recv_here, x_sem, y_sem,
 ):
     feat, node, size = lax.axis_index("feat"), lax.axis_index("nodes"), lax.axis_size("nodes")
     partner = {"feat": 1 - feat}
@@ -285,8 +303,17 @@
     barrier = pltpu.get_barrier_semaphore()
     first = [partner] + line_z + line_x + line_y
     signal_all(barrier, first)
+    loads = [
+        pltpu.make_async_copy(source, target, load_sems.at[i])
+        for i, (source, target) in enumerate(
+            [(own, mine), (enc.at[0], near_w.at[0]), (enc.at[1], near_w.at[1]), (dec.at[1], near_w.at[2])]
+        )
+    ]
+    for load in loads:
+        load.start()
     rows = grid.shape[0]
     pieces = rows // PIECE
+    per = PIECE // picked.shape[1]
     spot = lax.broadcasted_iota(jnp.int32, (rows, BLOCK), 0)
 
     def choose(c):
@@ -313,26 +340,26 @@
             pl.semaphore_wait(x_sem, len(line_x))
             signal_all(y_sem, line_y)
     pl.semaphore_wait(y_sem, len(line_y))
-    send_all(node, size, picked, arrived, send_sem, recv_sem)
-    weight = ordered(enc.at[1], feat)
+    send_all(node, size, picked, arrived, send_sem, recv_here)
+    for load in loads:
+        load.wait()
+    weight = ordered(near_w.at[1], feat)
     for c in range(pieces):
         copies[c].wait_recv()
         here = rows_of(c)
-        put(take, c, dot(jnp.concatenate([own[here, :], peer[here, :]], axis=1), weight))
+        put(take, c, dot(jnp.concatenate([mine[here, :], peer[here, :]], axis=1), weight))
     for copy in copies[pieces:]:
         copy.wait_recv()
     for copy in copies:
         copy.wait_send()
-    whole = drain(size, picked, arrived, send_sem, recv_sem, partner)
-    whole.wait_recv()
-    per = PIECE // arrived.shape[1]
+    drain(arrived, size - 1, send_sem, recv_here, partner).wait_recv()
     passes = [
         remote(arrived.at[pl.ds(c * per, per)], other.at[pl.ds(c * per, per)], grid_sends.at[c], grid_recvs.at[c], partner)
         for c in range(pieces)
     ]
     for copy in passes:
         copy.start()
-    first_w, second_w = ordered(enc.at[0], feat), ordered(dec.at[1], feat)
+    first_w, second_w = ordered(near_w.at[0], feat), ordered(near_w.at[2], feat)
     for c, copy in enumerate(passes):
         copy.wait_recv()
         both = jnp.concatenate([flat(arrived, c), flat(other, c)], axis=1)
@@ -340,7 +367,7 @@
         put(takes, c, dot(both, second_w))
     for copy in passes:
         copy.wait_send()
-    whole.wait_send()
+    drain(picked, size - 1, send_sem, recv_here, partner).wait_send()
 
 
 def start(order, grid, own, enc, mesh_w, dec, enc_gain, mesh_gain):
@@ -353,7 +380,7 @@
     regular = pltpu.SemaphoreType.REGULAR
     return call(
         start_kernel,
-        [VMEM] * 8,
+        [VMEM] * 2 + [HBM] * 6,
         [
             blocked,
             blocked,
@@ -363,15 +390,18 @@
             shape((1, width), F32),
             shape((ROUNDS, width), F32),
         ],
-        [split] * 3 + [DMA((count,))] * 2 + [DMA((pieces,))] * 2 + [DMA] * 2 + [regular] * 2,
+        [split] * 3
+        + [pltpu.VMEM((rows, width), BF16), pltpu.VMEM((3, D, width), BF16), DMA((4,))]
+        + [DMA((count,))] * 2 + [DMA((pieces,))] * 2 + [DMA] * 2 + [regular] * 2,
         collective_id=0,
+        limit=START_LIMIT,
         has_side_effects=True,
     )(order, grid, own, enc, mesh_w, dec, enc_gain, mesh_gain)
 
 
 def finish_kernel(
-    agg, dec, outer, gain, order, grid, out,
-    peer, update, returned, hot, landed, send_sems, recv_sems, send_sem, recv_sem, x_sem, y_sem,
+    agg, dec, outer, gain, order, out,
+    peer, update, returned, hot, landed, send_sems, recv_sems, send_sem, recv_here, x_sem, y_sem,
 ):
     feat, node, size = lax.axis_index("feat"), lax.axis_index("nodes"), lax.axis_size("nodes")
     partner = {"feat": 1 - feat}
@@ -380,12 +410,13 @@
     first = [partner] + line_z + line_x + line_y
     signal_all(barrier, first)
     pl.semaphore_wait(barrier, len(first))
+    signal_all(x_sem, line_x)
+    rows = agg.shape[0]
+    pieces = rows // PIECE
     copies = exchange(agg, peer, send_sems, recv_sems, partner)
     for copy in copies:
         copy.start()
-    signal_all(x_sem, line_x)
     mine, theirs = ordered(dec.at[2], feat), ordered(outer.at[1 + ROUNDS], feat)
-    pieces = len(copies)
     for c, copy in enumerate(copies):
         copy.wait_recv()
         here = rows_of(c)
@@ -396,24 +427,22 @@
             pl.semaphore_wait(x_sem, len(line_x))
             signal_all(y_sem, line_y)
     pl.semaphore_wait(y_sem, len(line_y))
-    send_all(node, size, update, returned, send_sem, recv_sem)
-    rows = grid.shape[0]
+    send_all(node, size, update, returned, send_sem, recv_here)
     for c in range(pieces):
-        spot = lax.broadcasted_iota(jnp.int32, (PIECE, rows), 0) + c * PIECE
-        hot[c * PIECE : (c + 1) * PIECE, :] = jnp.where(spot == order[...], 1.0, 0.0).astype(BF16)
+        hot_rows = lax.broadcasted_iota(jnp.int32, (PIECE, rows), 0) + c * PIECE
+        hot[c * PIECE : (c + 1) * PIECE, :] = jnp.where(hot_rows == order[...], 1.0, 0.0).astype(BF16)
     for copy in copies:
         copy.wait_send()
-    whole = drain(size, update, returned, send_sem, recv_sem, partner)
-    whole.wait_recv()
+    drain(returned, size - 1, send_sem, recv_here, partner).wait_recv()
     for c in range(pieces):
-        landed[c * PIECE : (c + 1) * PIECE, :] = flat(returned, c)
+        landed[rows_of(c), :] = flat(returned, c)
     for c in range(pieces):
         here = slice(c * PIECE, (c + 1) * PIECE)
-        out[here, :] = (grid[here, :].astype(F32) + dot(hot[here, :], landed[...])).astype(BF16)
-    whole.wait_send()
-
-
-def finish(agg, dec, outer, gain, order, grid):
+        out[here, :] = dot(hot[here, :], landed[...]).astype(BF16)
+    drain(update, size - 1, send_sem, recv_here, partner).wait_send()
+
+
+def finish(agg, dec, outer, gain, order):
     rows, width = agg.shape
     size = lax.axis_size("nodes")
     pieces = rows // PIECE
@@ -421,13 +450,13 @@
     regular = pltpu.SemaphoreType.REGULAR
     return call(
         finish_kernel,
-        [VMEM] * 6,
+        [VMEM] * 5,
         jax.ShapeDtypeStruct(agg.shape, BF16),
         [pltpu.VMEM((rows, width), BF16), split, split, pltpu.VMEM((rows, rows), BF16), pltpu.VMEM((rows, width), BF16)]
         + [DMA((pieces,))] * 2 + [DMA] * 2 + [regular] * 2,
         collective_id=6,
         has_side_effects=True,
-    )(agg, dec, outer, gain, order, grid)
+    )(agg, dec, outer, gain, order)
 
 
 def local(
@@ -484,11 +513,13 @@
         if not last:
             nearby, taking = sides
     (dec_send,) = sides
-    agg = edge_sum(
+    agg, mesh_own = edge_sum(
         dec_send, grid_take, dec_bias[None, :], 0, class_gain, 2,
-        dec_send_block, dec_recv_block, dec_offsets, dec_classes, dec_live, 12,
-    )
-    return (finish(agg, dec_weights, outer, dec_gain[None, :], grid_order, grid_latent), mesh_own)
+        dec_send_block, dec_recv_block, dec_offsets, dec_classes, dec_live, 12, mesh_own,
+    )
+    placed = finish(agg, dec_weights, outer, dec_gain[None, :], grid_order)
+    grid_out = (grid_latent.astype(F32) + placed.astype(F32)).astype(BF16)
+    return (grid_out, mesh_own)
 
 
 def solution(mesh):

time: 146 us -> 128 us (0.88)
  Pallas kernels: 139 us -> 118 us
  local copies, waits for them, and re-layouts: 2.67 us -> 4.48 us
    pallas_call x3, Pallas kernels: 53.1 us -> 41.2 us  [refresh(): call(functools.partial(refresh_kernel, near, stage, own_at, next_at, gain...]
    pallas_call x6, Pallas kernels: 86.2 us -> 76.9 us  [the longest x1 35.2 us: finish(): call(finish_kernel, [VMEM] * 5, jax.ShapeDtypeStruct(agg.shape, BF16), [p...]
    unnamed x4 -> x66, local copies, waits for them, and re-layouts: 2.67 us -> 4.48 us
where the time goes in v4:
time: 128 us; the launch traced here: 127 us
  Pallas kernels  118 us (92%)
  local copies, waits for them, and re-layouts  4.48 us (4%)
  between operations  3.31 us (3%)
    pallas_call x3, Pallas kernels, refresh(): call(functools.partial(refresh_kernel, near, stage, own_at, next_at, gain...  41.2 us
    pallas_call x1, Pallas kernels, finish(): call(finish_kernel, [VMEM] * 5, jax.ShapeDtypeStruct(agg.shape, BF16), [p...  35.2 us
    pallas_call x1, Pallas kernels, start(): call(start_kernel, [VMEM] * 2 + [HBM] * 6, [blocked, blocked, blocked, sh...  30.7 us
    pallas_call x3, Pallas kernels, edge_sum(): return call(kernel, specs, result, scratch)(*operands)  9.57 us
    unnamed x66, local copies, waits for them, and re-layouts  4.48 us

profile of v4, /device:TPU:2, one launch (start us, length us, event | category | flops | bytes accessed | tf_op | source)
XLA Modules:
  0.0 126.8 jit_solution(13115372316207916189)
XLA Ops:
  0.6 0.0 copy-start.12
  0.6 0.0 copy-start.15
  0.7 0.0 copy-start.19
  0.7 0.0 copy-start.27
  0.7 0.0 copy-start.28
  0.7 0.0 copy-start.29
  0.7 30.7 %shard_map.275 = (bf16[8,128,256]{2,1,0:T(8,128)(2,1)}, bf16[8,128,256]{2,1,0:T(8,128)(2,1)}, bf16[8,128,256]{2,1,0:T(8,128)(2,1)}, bf16[1024,256]{1,0:T(8,128)(...) custom-call(s32[1,1024]{1,0:T(1,128)} %order.3, bf16[1024,256]{1,0:T(8,128)(2,1)} %grid.1, ...), custom_call_target="tpu_custom_call" | custom-call | flops 268435456 | bytes 1048576 | tf_op jit(solution)/shard_map/pallas_call | solution.py:381
  31.4 0.0 copy-start
  32.2 1.0 copy-done.8
  33.3 1.0 copy-done.9
  34.3 2.0 %shard_map.276.agg = bf16[1024,256]{1,0:T(8,128)(2,1)S(1)} custom-call(s32[16]{0:T(128)S(1)} %copy-done.28, s32[16]{0:T(128)S(1)} %copy-done.29, s32[1]{0:T(128)S(6)} %copy.30.live, f32[3,8]{1,0:T(4,128)S(1)} %copy-done.12, s32[16,2,128]{2,1,0:T(2,128)S(1)} %copy-done.15, s32[16,128]{1,0:T(8,128)S(1)} %copy-done.19, f32[1,256]{1,0:T(1,128)S(1)} %bitcast.8, ...), custom_call_target="tpu_custom_call" | custom-call | flops 268435456 | bytes 1048576 | tf_op jit(solution)/shard_map/pallas_call | solution.py:104
  36.3 1.2 copy-done.1
  37.6 1.0 copy-done.6
  38.6 0.0 copy-start.23
  38.6 18.6 %shard_map.277 = (bf16[1024,256]{1,0:T(8,128)(2,1)S(1)}, bf16[1024,256]{1,0:T(8,128)(2,1)S(1)}, bf16[24,128,256]{2,1,0:T(8,128)(2,1)S(1)}, bf16[8,128,256]{2,1,0:T(8,128)(2,1)S(1)}) custom-call(bf16[1024,256]{1,0:T(8,128)(2,1)S(1)} %shard_map.276.agg, bf16[3,512,256]{2,1,0:T(8,128)(2,1)S(1)} %copy-done.4, bf16[4,512,256]{2,1,0:T(8,128)(2,1)S(1)} %copy-done.1, ...), custom_call_target="tpu_custom_call" | custom-call | flops 268435456 | bytes 1048576 | tf_op jit(solution)/shard_map/pallas_call | solution.py:230
  57.3 0.0 copy-start.14
  58.1 3.7 %shard_map.278.agg = bf16[1024,256]{1,0:T(8,128)(2,1)S(1)} custom-call(s32[96]{0:T(128)S(1)} %copy-done.22, s32[96]{0:T(128)S(1)} %copy-done.23, s32[1]{0:T(128)S(6)} %copy.31.live, f32[3,8]{1,0:T(4,128)S(1)} %copy-done.12, s32[96,2,128]{2,1,0:T(2,128)S(1)} %copy-done.10, s32[96,128]{1,0:T(8,128)S(1)} %copy-done.11, f32[2,256]{1,0:T(2,128)S(1)} %copy-done.20, ...), custom_call_target="tpu_custom_call" | custom-call | flops 268435456 | bytes 1048576 | tf_op jit(solution)/shard_map/pallas_call | solution.py:104
  61.8 17.6 %shard_map.279 = (bf16[1024,256]{1,0:T(8,128)(2,1)S(1)}, bf16[1024,256]{1,0:T(8,128)(2,1)S(1)}, bf16[24,128,256]{2,1,0:T(8,128)(2,1)S(1)}, bf16[8,128,256]{2,1,0:T(8,128)(2,1)S(1)}) custom-call(bf16[1024,256]{1,0:T(8,128)(2,1)S(1)} %shard_map.278.agg, bf16[2,3,512,256]{3,2,1,0:T(8,128)(2,1)S(1)} %copy-done, bf16[4,512,256]{2,1,0:T(8,128)(2,1)S(1)} %copy-done.2, ...), custom_call_target="tpu_custom_call" | custom-call | flops 268435456 | bytes 1048576 | tf_op jit(solution)/shard_map/pallas_call | solution.py:230
  79.4 0.0 copy-start.3
  79.4 3.9 %shard_map.280.agg = bf16[1024,256]{1,0:T(8,128)(2,1)S(1)} custom-call(s32[96]{0:T(128)S(1)} %copy-done.22, s32[96]{0:T(128)S(1)} %copy-done.23, s32[1]{0:T(128)S(6)} %copy.31.live, f32[3,8]{1,0:T(4,128)S(1)} %copy-done.12, s32[96,2,128]{2,1,0:T(2,128)S(1)} %copy-done.10, s32[96,128]{1,0:T(8,128)S(1)} %copy-done.11, f32[2,256]{1,0:T(2,128)S(1)} %copy-done.20, ...), custom_call_target="tpu_custom_call" | custom-call | flops 268435456 | bytes 1048576 | tf_op jit(solution)/shard_map/pallas_call | solution.py:104
  83.4 0.0 copy-start.13
  83.4 0.0 copy-start.17
  83.4 0.0 copy-start.24
  83.4 0.0 copy-start.30
  83.4 0.0 copy-start.31
  83.4 5.0 %shard_map.281 = (bf16[1024,256]{1,0:T(8,128)(2,1)S(1)}, bf16[1024,256]{1,0:T(8,128)(2,1)}, bf16[8,128,256]{2,1,0:T(8,128)(2,1)S(1)}) custom-call(bf16[1024,256]{1,0:T(8,128)(2,1)S(1)} %shard_map.280.agg, bf16[2,3,512,256]{3,2,1,0:T(8,128)(2,1)S(1)} %copy-done, bf16[4,512,256]{2,1,0:T(8,128)(2,1)S(1)} %copy-done.2, f32[2,256]{1,0:T(2,128)S(1)} %copy-done.14, ...), custom_call_target="tpu_custom_call" | custom-call | flops 268435456 | bytes 1048576 | tf_op jit(solution)/shard_map/pallas_call | solution.py:230
  88.4 0.0 copy-start.16
  88.4 0.0 copy-start.25
  89.1 1.5 %shard_map.282 = (bf16[1024,256]{1,0:T(8,128)(2,1)S(1)}, bf16[1024,256]{1,0:T(8,128)(2,1)}) custom-call(s32[24]{0:T(128)S(1)} %copy-done.30, s32[24]{0:T(128)S(1)} %copy-done.31, s32[1]{0:T(128)S(6)} %copy.32.live, f32[3,8]{1,0:T(4,128)S(1)} %copy-done.12, s32[24,2,128]{2,1,0:T(2,128)S(1)} %copy-done.13, s32[24,128]{1,0:T(8,128)S(1)} %copy-done.17, ...), custom_call_target="tpu_custom_call" | custom-call | flops 268435456 | bytes 1048576 | tf_op jit(solution)/shard_map/pallas_call | solution.py:106
  90.7 0.0 copy-start.32
  90.7 35.2 %shard_map.283 = bf16[1024,256]{1,0:T(8,128)(2,1)S(1)} custom-call(bf16[1024,256]{1,0:T(8,128)(2,1)S(1)} %get-tuple-element.38.agg, bf16[3,512,256]{2,1,0:T(8,128)(2,1)S(1)} %copy-done.3, bf16[4,512,256]{2,1,0:T(8,128)(2,1)S(1)} %copy-done.2, f32[1,256]{1,0:T(1,128)S(1)} %bitcast.7, s32[1,1024]{1,0:T(1,128)S(1)} %copy-done.16), custom_call_target="tpu_custom_call" | custom-call | flops 268435456 | bytes 1048576 | tf_op jit(solution)/shard_map/pallas_call | solution.py:451
  125.9 0.9 add_convert_fusion
  (44 shorter events, 0.1 us)
Async XLA Ops:
  0.6 31.5 %copy-start.12 = (f32[3,8]{1,0:T(4,128)S(1)}, f32[3,8]{1,0:T(4,128)}, u32[]{:S(2)}) copy-start(f32[3,8]{1,0:T(4,128)} %gains.7) | copy-start | bytes 292
  0.6 31.5 %copy-start.15 = (s32[16,2,128]{2,1,0:T(2,128)S(1)}, s32[16,2,128]{2,1,0:T(2,128)}, u32[]{:S(2)}) copy-start(s32[16,2,128]{2,1,0:T(2,128)} %offsets.4) | copy-start | bytes 49156
  0.7 31.5 %copy-start.19 = (s32[16,128]{1,0:T(8,128)S(1)}, s32[16,128]{1,0:T(8,128)}, u32[]{:S(2)}) copy-start(s32[16,128]{1,0:T(8,128)} %labels.4) | copy-start | bytes 24580
  0.7 31.5 %copy-start.27 = (f32[256]{0:T(256)S(1)}, f32[256]{0:T(256)}, u32[]{:S(2)}) copy-start(f32[256]{0:T(256)} %param.50) | copy-start | bytes 3076
  0.7 31.5 %copy-start.28 = (s32[16]{0:T(128)S(1)}, s32[16]{0:T(128)}, u32[]{:S(2)}) copy-start(s32[16]{0:T(128)} %send_ids.4) | copy-start | bytes 196
  0.7 31.5 %copy-start.29 = (s32[16]{0:T(128)S(1)}, s32[16]{0:T(128)}, u32[]{:S(2)}) copy-start(s32[16]{0:T(128)} %recv_ids.4) | copy-start | bytes 196
  0.7 35.6 %copy-start.4 = (bf16[3,512,256]{2,1,0:T(8,128)(2,1)S(1)}, bf16[3,512,256]{2,1,0:T(8,128)(2,1)}, u32[]{:S(2)}) copy-start(bf16[3,512,256]{2,1,0:T(8,128)(2,1)} %w_own.3) | copy-start | bytes 2359300
  0.7 35.6 %copy-start.5 = (bf16[1024,256]{1,0:T(8,128)(2,1)S(1)}, bf16[1024,256]{1,0:T(8,128)(2,1)}, u32[]{:S(2)}) copy-start(bf16[1024,256]{1,0:T(8,128)(2,1)} %mesh_own.1) | copy-start | bytes 1572868
  0.7 35.6 %copy-start.21 = (f32[256]{0:T(256)S(1)}, f32[256]{0:T(256)}, u32[]{:S(2)}) copy-start(f32[256]{0:T(256)} %param.51) | copy-start | bytes 3076
  31.4 4.9 %copy-start = (bf16[2,3,512,256]{3,2,1,0:T(8,128)(2,1)S(1)}, bf16[2,3,512,256]{3,2,1,0:T(8,128)(2,1)}, u32[]{:S(2)}) copy-start(bf16[2,3,512,256]{3,2,1,0:T(8,128)(2,1)} %w_own.5) | copy-start | bytes 4718596
  32.2 1.0 copy-start.8
  33.3 1.0 copy-start.9
  34.3 2.0 %copy-start.26 = (f32[1,256]{1,0:T(1,128)S(1)}, f32[1,256]{1,0:T(1,128)}, u32[]{:S(2)}) copy-start(f32[1,256]{1,0:T(1,128)} %get-tuple-element.24.gain_peer) | copy-start | bytes 3076
  36.3 1.2 copy-start.1
  38.6 19.4 %copy-start.10 = (s32[96,2,128]{2,1,0:T(2,128)S(1)}, s32[96,2,128]{2,1,0:T(2,128)}, u32[]{:S(2)}) copy-start(s32[96,2,128]{2,1,0:T(2,128)} %offsets.6) | copy-start | bytes 294916
  38.6 19.4 %copy-start.11 = (s32[96,128]{1,0:T(8,128)S(1)}, s32[96,128]{1,0:T(8,128)}, u32[]{:S(2)}) copy-start(s32[96,128]{1,0:T(8,128)} %labels.6) | copy-start | bytes 147460
  38.6 19.4 %copy-start.20 = (f32[2,256]{1,0:T(2,128)S(1)}, f32[2,256]{1,0:T(2,128)}, u32[]{:S(2)}) copy-start(f32[2,256]{1,0:T(2,128)} %bias.3) | copy-start | bytes 6148
  38.6 19.5 %copy-start.22 = (s32[96]{0:T(128)S(1)}, s32[96]{0:T(128)}, u32[]{:S(2)}) copy-start(s32[96]{0:T(128)} %send_ids.6) | copy-start | bytes 1156
  38.6 19.5 %copy-start.23 = (s32[96]{0:T(128)S(1)}, s32[96]{0:T(128)}, u32[]{:S(2)}) copy-start(s32[96]{0:T(128)} %recv_ids.6) | copy-start | bytes 1156
  57.3 4.5 %copy-start.2 = (bf16[4,512,256]{2,1,0:T(8,128)(2,1)S(1)}, bf16[4,512,256]{2,1,0:T(8,128)(2,1)}, u32[]{:S(2)}) copy-start(bf16[4,512,256]{2,1,0:T(8,128)(2,1)} %get-tuple-element.23.w_peer.outer) | copy-start | bytes 3145732
  57.3 4.5 %copy-start.14 = (f32[2,256]{1,0:T(2,128)S(1)}, f32[2,256]{1,0:T(2,128)}, u32[]{:S(2)}) copy-start(f32[2,256]{1,0:T(2,128)} %gain_own.3) | copy-start | bytes 6148
  57.3 4.5 %copy-start.18 = (f32[2,256]{1,0:T(2,128)S(1)}, f32[2,256]{1,0:T(2,128)}, u32[]{:S(2)}) copy-start(f32[2,256]{1,0:T(2,128)} %get-tuple-element.28.gain_peer) | copy-start | bytes 6148
  79.4 3.9 %copy-start.3 = (bf16[3,512,256]{2,1,0:T(8,128)(2,1)S(1)}, bf16[3,512,256]{2,1,0:T(8,128)(2,1)}, u32[]{:S(2)}) copy-start(bf16[3,512,256]{2,1,0:T(8,128)(2,1)} %dec.3) | copy-start | bytes 2359300
  83.3 5.7 %copy-start.7 = (bf16[8,128,256]{2,1,0:T(8,128)(2,1)S(1)}, bf16[8,128,256]{2,1,0:T(8,128)(2,1)}, u32[]{:S(2)}) copy-start(bf16[8,128,256]{2,1,0:T(8,128)(2,1)} %get-tuple-element.36.receiver) | copy-start | bytes 1572868
  83.4 5.7 %copy-start.13 = (s32[24,2,128]{2,1,0:T(2,128)S(1)}, s32[24,2,128]{2,1,0:T(2,128)}, u32[]{:S(2)}) copy-start(s32[24,2,128]{2,1,0:T(2,128)} %offsets.7) | copy-start | bytes 73732
  83.4 5.7 %copy-start.17 = (s32[24,128]{1,0:T(8,128)S(1)}, s32[24,128]{1,0:T(8,128)}, u32[]{:S(2)}) copy-start(s32[24,128]{1,0:T(8,128)} %labels.7) | copy-start | bytes 36868
  83.4 5.7 %copy-start.24 = (f32[256]{0:T(256)S(1)}, f32[256]{0:T(256)}, u32[]{:S(2)}) copy-start(f32[256]{0:T(256)} %param.54) | copy-start | bytes 3076
  83.4 5.7 %copy-start.30 = (s32[24]{0:T(128)S(1)}, s32[24]{0:T(128)}, u32[]{:S(2)}) copy-start(s32[24]{0:T(128)} %send_ids.7) | copy-start | bytes 292
  83.4 5.7 %copy-start.31 = (s32[24]{0:T(128)S(1)}, s32[24]{0:T(128)}, u32[]{:S(2)}) copy-start(s32[24]{0:T(128)} %recv_ids.7) | copy-start | bytes 292
  88.4 2.3 %copy-start.16 = (s32[1,1024]{1,0:T(1,128)S(1)}, s32[1,1024]{1,0:T(1,128)}, u32[]{:S(2)}) copy-start(s32[1,1024]{1,0:T(1,128)} %order.3) | copy-start | bytes 12292
  88.4 2.3 %copy-start.25 = (f32[256]{0:T(256)S(1)}, f32[256]{0:T(256)}, u32[]{:S(2)}) copy-start(f32[256]{0:T(256)} %param.55) | copy-start | bytes 3076
  90.7 35.2 %copy-start.32 = (bf16[1024,256]{1,0:T(8,128)(2,1)S(1)}, bf16[1024,256]{1,0:T(8,128)(2,1)}, u32[]{:S(2)}) copy-start(bf16[1024,256]{1,0:T(8,128)(2,1)} %grid.1) | copy-start | bytes 1572868
  (1 other events, 1.0 us)

commit v5 on v4

--- a/solution.py
+++ b/solution.py
@@ -261,11 +261,13 @@
         pl.semaphore_signal(semaphore, inc=1, device_id=partner, device_id_type=MESH_ID)
 
 
-def send_all(node, size, source, target, send_sem, recv_sem):
+def send_some(node, size, group, source, target, send_sem, recv_sem):
     z, x, y = extents(size)
+    stride = (1, z, z * x)[group]
+    count = (z, x, y)[group] * stride
 
     def send(i, carry):
-        j = size - i
+        j = count - 1 - i
         to_z = lax.rem(node // (x * y) + lax.rem(j, z), z)
         to_x = lax.rem((node // y) % x + lax.rem(j // z, x), x)
         to_y = lax.rem(node % y + j // (z * x), y)
@@ -273,8 +275,7 @@
         remote(source.at[to], target.at[node], send_sem, recv_sem, {"nodes": to}).start()
         return carry
 
-    lax.fori_loop(1, size, send, 0)
-    target[pl.ds(node, 1)] = source[pl.ds(node, 1)]
+    lax.fori_loop(0, count - stride, send, 0)
 
 
 def drain(ref, count, send_sem, recv_sem, partner):
@@ -331,16 +332,17 @@
 
     for c in range(pieces):
         choose(c)
-        if c == pieces // 2 - 1:
-            pl.semaphore_wait(barrier, len(first))
-            signal_all(x_sem, line_x)
-            for copy in copies:
-                copy.start()
-        if c == pieces - 2:
-            pl.semaphore_wait(x_sem, len(line_x))
-            signal_all(y_sem, line_y)
+    pl.semaphore_wait(barrier, len(first))
+    signal_all(x_sem, line_x)
+    send_some(node, size, 0, picked, arrived, send_sem, recv_here)
+    for copy in copies:
+        copy.start()
+    pl.semaphore_wait(x_sem, len(line_x))
+    signal_all(y_sem, line_y)
+    send_some(node, size, 1, picked, arrived, send_sem, recv_here)
     pl.semaphore_wait(y_sem, len(line_y))
-    send_all(node, size, picked, arrived, send_sem, recv_here)
+    send_some(node, size, 2, picked, arrived, send_sem, recv_here)
+    arrived[pl.ds(node, 1)] = picked[pl.ds(node, 1)]
     for load in loads:
         load.wait()
     weight = ordered(near_w.at[1], feat)
@@ -360,8 +362,9 @@
     for copy in passes:
         copy.start()
     first_w, second_w = ordered(near_w.at[0], feat), ordered(near_w.at[2], feat)
-    for c, copy in enumerate(passes):
+    for copy in passes:
         copy.wait_recv()
+    for c in range(pieces):
         both = jnp.concatenate([flat(arrived, c), flat(other, c)], axis=1)
         put(sides, c, dot(both, first_w))
         put(takes, c, dot(both, second_w))
@@ -417,17 +420,20 @@
     for copy in copies:
         copy.start()
     mine, theirs = ordered(dec.at[2], feat), ordered(outer.at[1 + ROUNDS], feat)
-    for c, copy in enumerate(copies):
+    for copy in copies:
         copy.wait_recv()
+    pl.semaphore_wait(x_sem, len(line_x))
+    signal_all(y_sem, line_y)
+    for c in range(pieces):
         here = rows_of(c)
         both = jnp.concatenate([agg[here, :], peer[here, :]], axis=1)
         fresh, _ = normed(dot(both, mine), dot(both, theirs), gain[...], None)
         put_split(update, c, fresh)
-        if c == pieces // 2 - 1:
-            pl.semaphore_wait(x_sem, len(line_x))
-            signal_all(y_sem, line_y)
+    send_some(node, size, 0, update, returned, send_sem, recv_here)
+    send_some(node, size, 1, update, returned, send_sem, recv_here)
     pl.semaphore_wait(y_sem, len(line_y))
-    send_all(node, size, update, returned, send_sem, recv_here)
+    send_some(node, size, 2, update, returned, send_sem, recv_here)
+    returned[pl.ds(node, 1)] = update[pl.ds(node, 1)]
     for c in range(pieces):
         hot_rows = lax.broadcasted_iota(jnp.int32, (PIECE, rows), 0) + c * PIECE
         hot[c * PIECE : (c + 1) * PIECE, :] = jnp.where(hot_rows == order[...], 1.0, 0.0).astype(BF16)

time: 128 us -> 127 us (level); the launches traced: 127 us -> 124 us
  Pallas kernels: 118 us -> 116 us
    pallas_call x1, Pallas kernels: 35.2 us -> 27.7 us  [finish(): call(finish_kernel, [VMEM] * 5, jax.ShapeDtypeStruct(agg.shape, BF16), [p...]
    pallas_call x3, Pallas kernels: 9.57 us -> 14.9 us  [edge_sum(): return call(kernel, specs, result, scratch)(*operands)]
where the time goes in v5:
time: 127 us; the launch traced here: 124 us
  Pallas kernels  116 us (91%)
  local copies, waits for them, and re-layouts  4.48 us (4%)
  between operations  3.31 us (3%)
    pallas_call x3, Pallas kernels, refresh(): call(functools.partial(refresh_kernel, near, stage, own_at, next_at, gain...  41.2 us
    pallas_call x1, Pallas kernels, start(): call(start_kernel, [VMEM] * 2 + [HBM] * 6, [blocked, blocked, blocked, sh...  29.5 us
    pallas_call x1, Pallas kernels, finish(): call(finish_kernel, [VMEM] * 5, jax.ShapeDtypeStruct(agg.shape, BF16), [p...  27.7 us
    pallas_call x3, Pallas kernels, edge_sum(): return call(kernel, specs, result, scratch)(*operands)  14.9 us
    unnamed x66, local copies, waits for them, and re-layouts  4.48 us

profile of v5, /device:TPU:2, one launch (start us, length us, event | category | flops | bytes accessed | tf_op | source)
XLA Modules:
  0.0 124.3 jit_solution(12823303164798800191)
XLA Ops:
  0.7 29.5 %shard_map.275 = (bf16[8,128,256]{2,1,0:T(8,128)(2,1)}, bf16[8,128,256]{2,1,0:T(8,128)(2,1)}, bf16[8,128,256]{2,1,0:T(8,128)(2,1)}, bf16[1024,256]{1,0:T(8,128)(...) custom-call(s32[1,1024]{1,0:T(1,128)} %order.3, bf16[1024,256]{1,0:T(8,128)(2,1)} %grid.1, ...), custom_call_target="tpu_custom_call" | custom-call | flops 268435456 | bytes 1048576 | tf_op jit(solution)/shard_map/pallas_call | solution.py:384
  30.3 0.0 copy-start
  31.1 1.0 copy-done.8
  32.2 1.0 copy-done.9
  33.2 1.3 %shard_map.276.agg = bf16[1024,256]{1,0:T(8,128)(2,1)S(1)} custom-call(s32[16]{0:T(128)S(1)} %copy-done.28, s32[16]{0:T(128)S(1)} %copy-done.29, s32[1]{0:T(128)S(6)} %copy.30.live, f32[3,8]{1,0:T(4,128)S(1)} %copy-done.12, s32[16,2,128]{2,1,0:T(2,128)S(1)} %copy-done.15, s32[16,128]{1,0:T(8,128)S(1)} %copy-done.19, f32[1,256]{1,0:T(1,128)S(1)} %bitcast.8, ...), custom_call_target="tpu_custom_call" | custom-call | flops 268435456 | bytes 1048576 | tf_op jit(solution)/shard_map/pallas_call | solution.py:104
  34.5 0.0 copy-done.4
  34.6 0.0 copy-done.5
  34.6 0.0 copy-done.21
  34.6 0.0 copy-done
  34.6 0.0 copy-done.26
  34.6 0.0 copy-start.1
  34.6 1.2 copy-done.1
  35.8 1.0 copy-done.6
  36.9 0.0 copy-start.23
  36.9 18.6 %shard_map.277 = (bf16[1024,256]{1,0:T(8,128)(2,1)S(1)}, bf16[1024,256]{1,0:T(8,128)(2,1)S(1)}, bf16[24,128,256]{2,1,0:T(8,128)(2,1)S(1)}, bf16[8,128,256]{2,1,0:T(8,128)(2,1)S(1)}) custom-call(bf16[1024,256]{1,0:T(8,128)(2,1)S(1)} %shard_map.276.agg, bf16[3,512,256]{2,1,0:T(8,128)(2,1)S(1)} %copy-done.4, bf16[4,512,256]{2,1,0:T(8,128)(2,1)S(1)} %copy-done.1, ...), custom_call_target="tpu_custom_call" | custom-call | flops 268435456 | bytes 1048576 | tf_op jit(solution)/shard_map/pallas_call | solution.py:230
  55.5 0.0 copy-start.14
  56.3 6.7 %shard_map.278.agg = bf16[1024,256]{1,0:T(8,128)(2,1)S(1)} custom-call(s32[96]{0:T(128)S(1)} %copy-done.22, s32[96]{0:T(128)S(1)} %copy-done.23, s32[1]{0:T(128)S(6)} %copy.31.live, f32[3,8]{1,0:T(4,128)S(1)} %copy-done.12, s32[96,2,128]{2,1,0:T(2,128)S(1)} %copy-done.10, s32[96,128]{1,0:T(8,128)S(1)} %copy-done.11, f32[2,256]{1,0:T(2,128)S(1)} %copy-done.20, ...), custom_call_target="tpu_custom_call" | custom-call | flops 268435456 | bytes 1048576 | tf_op jit(solution)/shard_map/pallas_call | solution.py:104
  63.0 17.6 %shard_map.279 = (bf16[1024,256]{1,0:T(8,128)(2,1)S(1)}, bf16[1024,256]{1,0:T(8,128)(2,1)S(1)}, bf16[24,128,256]{2,1,0:T(8,128)(2,1)S(1)}, bf16[8,128,256]{2,1,0:T(8,128)(2,1)S(1)}) custom-call(bf16[1024,256]{1,0:T(8,128)(2,1)S(1)} %shard_map.278.agg, bf16[2,3,512,256]{3,2,1,0:T(8,128)(2,1)S(1)} %copy-done, bf16[4,512,256]{2,1,0:T(8,128)(2,1)S(1)} %copy-done.2, ...), custom_call_target="tpu_custom_call" | custom-call | flops 268435456 | bytes 1048576 | tf_op jit(solution)/shard_map/pallas_call | solution.py:230
  80.6 0.0 copy-start.3
  80.6 6.9 %shard_map.280.agg = bf16[1024,256]{1,0:T(8,128)(2,1)S(1)} custom-call(s32[96]{0:T(128)S(1)} %copy-done.22, s32[96]{0:T(128)S(1)} %copy-done.23, s32[1]{0:T(128)S(6)} %copy.31.live, f32[3,8]{1,0:T(4,128)S(1)} %copy-done.12, s32[96,2,128]{2,1,0:T(2,128)S(1)} %copy-done.10, s32[96,128]{1,0:T(8,128)S(1)} %copy-done.11, f32[2,256]{1,0:T(2,128)S(1)} %copy-done.20, ...), custom_call_target="tpu_custom_call" | custom-call | flops 268435456 | bytes 1048576 | tf_op jit(solution)/shard_map/pallas_call | solution.py:104
  87.6 0.0 copy-start.13
  87.6 0.0 copy-start.17
  87.6 0.0 copy-start.24
  87.6 0.0 copy-start.30
  87.6 0.0 copy-start.31
  87.6 5.0 %shard_map.281 = (bf16[1024,256]{1,0:T(8,128)(2,1)S(1)}, bf16[1024,256]{1,0:T(8,128)(2,1)}, bf16[8,128,256]{2,1,0:T(8,128)(2,1)S(1)}) custom-call(bf16[1024,256]{1,0:T(8,128)(2,1)S(1)} %shard_map.280.agg, bf16[2,3,512,256]{3,2,1,0:T(8,128)(2,1)S(1)} %copy-done, bf16[4,512,256]{2,1,0:T(8,128)(2,1)S(1)} %copy-done.2, f32[2,256]{1,0:T(2,128)S(1)} %copy-done.14, ...), custom_call_target="tpu_custom_call" | custom-call | flops 268435456 | bytes 1048576 | tf_op jit(solution)/shard_map/pallas_call | solution.py:230
  92.6 0.0 copy-start.16
  92.6 0.0 copy-start.25
  93.4 2.3 %shard_map.282 = (bf16[1024,256]{1,0:T(8,128)(2,1)S(1)}, bf16[1024,256]{1,0:T(8,128)(2,1)}) custom-call(s32[24]{0:T(128)S(1)} %copy-done.30, s32[24]{0:T(128)S(1)} %copy-done.31, s32[1]{0:T(128)S(6)} %copy.32.live, f32[3,8]{1,0:T(4,128)S(1)} %copy-done.12, s32[24,2,128]{2,1,0:T(2,128)S(1)} %copy-done.13, s32[24,128]{1,0:T(8,128)S(1)} %copy-done.17, ...), custom_call_target="tpu_custom_call" | custom-call | flops 268435456 | bytes 1048576 | tf_op jit(solution)/shard_map/pallas_call | solution.py:106
  95.7 0.0 copy-start.32
  95.7 27.7 %shard_map.283 = bf16[1024,256]{1,0:T(8,128)(2,1)S(1)} custom-call(bf16[1024,256]{1,0:T(8,128)(2,1)S(1)} %get-tuple-element.38.agg, bf16[3,512,256]{2,1,0:T(8,128)(2,1)S(1)} %copy-done.3, bf16[4,512,256]{2,1,0:T(8,128)(2,1)S(1)} %copy-done.2, f32[1,256]{1,0:T(1,128)S(1)} %bitcast.7, s32[1,1024]{1,0:T(1,128)S(1)} %copy-done.16), custom_call_target="tpu_custom_call" | custom-call | flops 268435456 | bytes 1048576 | tf_op jit(solution)/shard_map/pallas_call | solution.py:457
  123.4 0.9 add_convert_fusion
  (44 shorter events, 0.1 us)
Async XLA Ops:
  0.6 30.4 %copy-start.12 = (f32[3,8]{1,0:T(4,128)S(1)}, f32[3,8]{1,0:T(4,128)}, u32[]{:S(2)}) copy-start(f32[3,8]{1,0:T(4,128)} %gains.7) | copy-start | bytes 292
  0.6 30.4 %copy-start.15 = (s32[16,2,128]{2,1,0:T(2,128)S(1)}, s32[16,2,128]{2,1,0:T(2,128)}, u32[]{:S(2)}) copy-start(s32[16,2,128]{2,1,0:T(2,128)} %offsets.4) | copy-start | bytes 49156
  0.7 30.4 %copy-start.19 = (s32[16,128]{1,0:T(8,128)S(1)}, s32[16,128]{1,0:T(8,128)}, u32[]{:S(2)}) copy-start(s32[16,128]{1,0:T(8,128)} %labels.4) | copy-start | bytes 24580
  0.7 30.4 %copy-start.27 = (f32[256]{0:T(256)S(1)}, f32[256]{0:T(256)}, u32[]{:S(2)}) copy-start(f32[256]{0:T(256)} %param.50) | copy-start | bytes 3076
  0.7 30.4 %copy-start.28 = (s32[16]{0:T(128)S(1)}, s32[16]{0:T(128)}, u32[]{:S(2)}) copy-start(s32[16]{0:T(128)} %send_ids.4) | copy-start | bytes 196
  0.7 30.4 %copy-start.29 = (s32[16]{0:T(128)S(1)}, s32[16]{0:T(128)}, u32[]{:S(2)}) copy-start(s32[16]{0:T(128)} %recv_ids.4) | copy-start | bytes 196
  0.7 33.8 %copy-start.4 = (bf16[3,512,256]{2,1,0:T(8,128)(2,1)S(1)}, bf16[3,512,256]{2,1,0:T(8,128)(2,1)}, u32[]{:S(2)}) copy-start(bf16[3,512,256]{2,1,0:T(8,128)(2,1)} %w_own.3) | copy-start | bytes 2359300
  0.7 33.8 %copy-start.5 = (bf16[1024,256]{1,0:T(8,128)(2,1)S(1)}, bf16[1024,256]{1,0:T(8,128)(2,1)}, u32[]{:S(2)}) copy-start(bf16[1024,256]{1,0:T(8,128)(2,1)} %mesh_own.1) | copy-start | bytes 1572868
  0.7 33.8 %copy-start.21 = (f32[256]{0:T(256)S(1)}, f32[256]{0:T(256)}, u32[]{:S(2)}) copy-start(f32[256]{0:T(256)} %param.51) | copy-start | bytes 3076
  30.3 4.3 %copy-start = (bf16[2,3,512,256]{3,2,1,0:T(8,128)(2,1)S(1)}, bf16[2,3,512,256]{3,2,1,0:T(8,128)(2,1)}, u32[]{:S(2)}) copy-start(bf16[2,3,512,256]{3,2,1,0:T(8,128)(2,1)} %w_own.5) | copy-start | bytes 4718596
  31.1 1.0 copy-start.8
  32.2 1.0 copy-start.9
  33.2 1.4 %copy-start.26 = (f32[1,256]{1,0:T(1,128)S(1)}, f32[1,256]{1,0:T(1,128)}, u32[]{:S(2)}) copy-start(f32[1,256]{1,0:T(1,128)} %get-tuple-element.24.gain_peer) | copy-start | bytes 3076
  34.6 1.2 copy-start.1
  36.9 19.4 %copy-start.10 = (s32[96,2,128]{2,1,0:T(2,128)S(1)}, s32[96,2,128]{2,1,0:T(2,128)}, u32[]{:S(2)}) copy-start(s32[96,2,128]{2,1,0:T(2,128)} %offsets.6) | copy-start | bytes 294916
  36.9 19.4 %copy-start.11 = (s32[96,128]{1,0:T(8,128)S(1)}, s32[96,128]{1,0:T(8,128)}, u32[]{:S(2)}) copy-start(s32[96,128]{1,0:T(8,128)} %labels.6) | copy-start | bytes 147460
  36.9 19.4 %copy-start.20 = (f32[2,256]{1,0:T(2,128)S(1)}, f32[2,256]{1,0:T(2,128)}, u32[]{:S(2)}) copy-start(f32[2,256]{1,0:T(2,128)} %bias.3) | copy-start | bytes 6148
  36.9 19.5 %copy-start.22 = (s32[96]{0:T(128)S(1)}, s32[96]{0:T(128)}, u32[]{:S(2)}) copy-start(s32[96]{0:T(128)} %send_ids.6) | copy-start | bytes 1156
  36.9 19.5 %copy-start.23 = (s32[96]{0:T(128)S(1)}, s32[96]{0:T(128)}, u32[]{:S(2)}) copy-start(s32[96]{0:T(128)} %recv_ids.6) | copy-start | bytes 1156
  55.5 7.5 %copy-start.2 = (bf16[4,512,256]{2,1,0:T(8,128)(2,1)S(1)}, bf16[4,512,256]{2,1,0:T(8,128)(2,1)}, u32[]{:S(2)}) copy-start(bf16[4,512,256]{2,1,0:T(8,128)(2,1)} %get-tuple-element.23.w_peer.outer) | copy-start | bytes 3145732
  55.5 7.5 %copy-start.14 = (f32[2,256]{1,0:T(2,128)S(1)}, f32[2,256]{1,0:T(2,128)}, u32[]{:S(2)}) copy-start(f32[2,256]{1,0:T(2,128)} %gain_own.3) | copy-start | bytes 6148
  55.5 7.5 %copy-start.18 = (f32[2,256]{1,0:T(2,128)S(1)}, f32[2,256]{1,0:T(2,128)}, u32[]{:S(2)}) copy-start(f32[2,256]{1,0:T(2,128)} %get-tuple-element.28.gain_peer) | copy-start | bytes 6148
  80.6 6.9 %copy-start.3 = (bf16[3,512,256]{2,1,0:T(8,128)(2,1)S(1)}, bf16[3,512,256]{2,1,0:T(8,128)(2,1)}, u32[]{:S(2)}) copy-start(bf16[3,512,256]{2,1,0:T(8,128)(2,1)} %dec.3) | copy-start | bytes 2359300
  87.6 5.7 %copy-start.7 = (bf16[8,128,256]{2,1,0:T(8,128)(2,1)S(1)}, bf16[8,128,256]{2,1,0:T(8,128)(2,1)}, u32[]{:S(2)}) copy-start(bf16[8,128,256]{2,1,0:T(8,128)(2,1)} %get-tuple-element.36.receiver) | copy-start | bytes 1572868
  87.6 5.7 %copy-start.13 = (s32[24,2,128]{2,1,0:T(2,128)S(1)}, s32[24,2,128]{2,1,0:T(2,128)}, u32[]{:S(2)}) copy-start(s32[24,2,128]{2,1,0:T(2,128)} %offsets.7) | copy-start | bytes 73732
  87.6 5.7 %copy-start.17 = (s32[24,128]{1,0:T(8,128)S(1)}, s32[24,128]{1,0:T(8,128)}, u32[]{:S(2)}) copy-start(s32[24,128]{1,0:T(8,128)} %labels.7) | copy-start | bytes 36868
  87.6 5.7 %copy-start.24 = (f32[256]{0:T(256)S(1)}, f32[256]{0:T(256)}, u32[]{:S(2)}) copy-start(f32[256]{0:T(256)} %param.54) | copy-start | bytes 3076
  87.6 5.7 %copy-start.30 = (s32[24]{0:T(128)S(1)}, s32[24]{0:T(128)}, u32[]{:S(2)}) copy-start(s32[24]{0:T(128)} %send_ids.7) | copy-start | bytes 292
  87.6 5.7 %copy-start.31 = (s32[24]{0:T(128)S(1)}, s32[24]{0:T(128)}, u32[]{:S(2)}) copy-start(s32[24]{0:T(128)} %recv_ids.7) | copy-start | bytes 292
  92.6 3.1 %copy-start.16 = (s32[1,1024]{1,0:T(1,128)S(1)}, s32[1,1024]{1,0:T(1,128)}, u32[]{:S(2)}) copy-start(s32[1,1024]{1,0:T(1,128)} %order.3) | copy-start | bytes 12292
  92.6 3.1 %copy-start.25 = (f32[256]{0:T(256)S(1)}, f32[256]{0:T(256)}, u32[]{:S(2)}) copy-start(f32[256]{0:T(256)} %param.55) | copy-start | bytes 3076
  95.7 27.7 %copy-start.32 = (bf16[1024,256]{1,0:T(8,128)(2,1)S(1)}, bf16[1024,256]{1,0:T(8,128)(2,1)}, u32[]{:S(2)}) copy-start(bf16[1024,256]{1,0:T(8,128)(2,1)} %grid.1) | copy-start | bytes 1572868
  (1 other events, 1.0 us)
